TPU v7x, 8 devices: a whole 2x2x1 slice. The times are simulated.
8 devices in a mesh: dp: 2 (over y, z), tp: 4 (over x, core).
Axes of the slice: x: 2, y: 2, z: 1, core: 2. Of those that a mesh axis runs over, the one named last changes fastest.
Arguments:
- x: bfloat16 [256, 4096], P('dp'), parts along dimension 0
- w_gate: bfloat16 [4096, 16384], P(None, 'tp')
- w_up: bfloat16 [4096, 16384], P(None, 'tp')
- w_down: bfloat16 [16384, 4096], P('tp')
Outputs:
- output: bfloat16 [256, 4096], P('dp'), parts along dimension 0
There are 2 independent parts. A program takes and returns all parts, laid end to end along the dimension named above; an argument that names none is the same for every part.
All inputs are finite; a program needn't handle non-finite values.
Results may differ from a plain program's by a relative error of at most 0.016.
Values are sent between devices in bfloat16 or wider.
A program may use at most 2 GiB of HBM per device.

v0:
```python
import jax
import jax.numpy as jnp
from jax import lax
from jax.sharding import PartitionSpec as P


def solution(mesh):
    def step(x, w_gate, w_up, w_down):
        gate = jnp.dot(x, w_gate, preferred_element_type=jnp.float32)
        up = jnp.dot(x, w_up, preferred_element_type=jnp.float32)
        hidden = (jax.nn.silu(gate) * up).astype(jnp.bfloat16)
        term = jnp.dot(hidden, w_down, preferred_element_type=jnp.float32).astype(jnp.bfloat16)
        return lax.psum(term, "tp")

    return jax.shard_map(
        step,
        mesh=mesh,
        in_specs=(P("dp", None), P(None, "tp"), P(None, "tp"), P("tp", None)),
        out_specs=P("dp", None),
        check_vma=False,
    )
```

profile of v0, /device:TPU:0, one launch (start us, length us, event | category | flops | bytes accessed | tf_op | source)
XLA Modules:
  0.0 88.7 jit_solution(6306702679745724074)
XLA Ops:
  6.5 0.0 copy-start
  6.5 0.0 all-reduce.2.cloned.1.call-start
  6.5 1.2 %copy-done = bf16[128,4096]{1,0:T(8,128)(2,1)S(1)} copy-done((bf16[128,4096]{1,0:T(8,128)(2,1)S(1)}, bf16[128,4096]{1,0:T(8,128)(2,1)}, u32[]{:S(2)}) %copy-start) | copy-done | bytes 1048600
  7.8 12.9 %fusion.8 = f32[128,4096]{1,0:T(8,128)S(1)} fusion(bf16[128,4096]{1,0:T(8,128)(2,1)S(1)} %copy-done, bf16[4096,4096]{1,0:T(8,128)(2,1)} %param.5), kind=kOutput, calls=%fused_computation.10 | convolution fusion | flops 4294967296 | bytes 36700160 | tf_op jit(solution)/shard_map/dot_general | solution.py:9
  20.7 25.1 %convolution_convert_fusion = bf16[128,4096]{1,0:T(8,128)(2,1)} fusion(bf16[4096,4096]{1,0:T(8,128)(2,1)} %param.7, bf16[128,4096]{1,0:T(8,128)(2,1)S(1)} %copy-done, bf16[4096,4096]{1,0:T(8,128)(2,1)} %param.6, f32[128,4096]{1,0:T(8,128)S(1)} %fusion.8), kind=kOutput, calls=%fused_computation.2 | convolution fusion | flops 8593604608 | bytes 71303168 | tf_op jit(solution)/shard_map/dot_general | solution.py:12
  45.7 0.0 all-reduce.2.cloned.1.call-update
  45.8 33.8 %all-reduce.2.cloned.1.call-done = bf16[128,4096]{1,0:T(8,128)(2,1)} async-done(((bf16[128,4096]{1,0:T(8,128)(2,1)}), bf16[128,4096]{1,0:T(8,128)(2,1)}) %all-reduce.2.cloned.1.call-update) | async-done | bytes 1048592 | tf_op jit(solution)/shard_map/psum | solution.py:13
  79.6 2.3 %copy.6 = bf16[128,4096]{1,0:T(8,128)(2,1)} copy(bf16[128,4096]{1,0:T(8,128)(2,1)} %all-reduce.2.cloned.1.call-done) | data formatting | bytes 2097152
Async XLA Ops:
  6.5 1.2 %copy-start = (bf16[128,4096]{1,0:T(8,128)(2,1)S(1)}, bf16[128,4096]{1,0:T(8,128)(2,1)}, u32[]{:S(2)}) copy-start(bf16[128,4096]{1,0:T(8,128)(2,1)} %param.4) | copy-start | bytes 3145732
  6.5 73.0 %all-reduce.2.cloned.1.call-start = ((), (), s32[]{:S(2)}) async-start(), calls=%async_computation | async-start | bytes 2097152 | tf_op jit(solution)/shard_map/psum | solution.py:13
Sparse Core Ops, SparseCore 0:
  45.9 33.6 all-reduce.1
where the time goes:
time: 88.9 us; the launch traced here: 88.7 us
  matrix products  38 us (43%)
  waiting for transfers between devices  33.8 us (38%)
  between operations  13.4 us (15%)
  local copies, waits for them, and re-layouts  3.51 us (4%)
    psum x1, waiting for transfers between devices, step(): return lax.psum(term, 'tp')  33.8 us
    dot_general x1, matrix products, step(): jnp.dot(hidden, w_down, preferred_element_type=jnp.float32)  25.1 us
    dot_general x1, matrix products, step(): gate = jnp.dot(x, w_gate, preferred_element_type=jnp.float32)  12.9 us
    unnamed x3, local copies, waits for them, and re-layouts  3.51 us
  transfers between devices with their start and end apart: 1, of which 1 were waited for; matrix products, arithmetic and copies ran while one was open for 0% of the time, Pallas kernels for 0%

commit v1 on v0

v1 whole, which is shorter than its diff:
```python
import functools

import jax
import jax.numpy as jnp
from jax import lax
from jax.experimental import pallas as pl
from jax.experimental.pallas import tpu as pltpu
from jax.sharding import PartitionSpec as P

MESH = pl.DeviceIdType.MESH
ROWS = 128
HALF = ROWS // 2
D = 4096
F = 4096
BN = 256
SLOTS = 8
NG = F // BN
DB = 2 * BN
ND = D // DB
LAG_X = 1
LAG_Y = 4


def kernel(x_hbm, wg_hbm, wu_hbm, wd_hbm, y_ref,
           xv, h, w, tb, tf, rb, ub, xr, x_sem, w_sem,
           d_send, d_recv, u_send, u_recv, g_send, g_recv):
    tp = lax.axis_index("tp")
    core = lax.rem(tp, 2)
    chip = tp // 2
    partner = {"tp": 2 * chip + (1 - core)}
    across = {"tp": 2 * (1 - chip) + core}
    mine = pl.ds(pl.multiple_of(core * HALF, HALF), HALF)
    theirs = pl.ds(pl.multiple_of((1 - core) * HALF, HALF), HALF)

    def gu_copies(i, s):
        cols = pl.ds(pl.multiple_of(i * BN, BN), BN)
        return (pltpu.make_async_copy(wg_hbm.at[:, cols], w.at[s, 0], w_sem.at[s, 0]),
                pltpu.make_async_copy(wu_hbm.at[:, cols], w.at[s, 1], w_sem.at[s, 1]))

    def d_copies(j, s):
        return tuple(
            pltpu.make_async_copy(
                wd_hbm.at[:, pl.ds(pl.multiple_of(j * DB + q * BN, BN), BN)], w.at[s, q], w_sem.at[s, q])
            for q in range(2))

    x_copy = pltpu.make_async_copy(x_hbm, xv, x_sem)
    x_copy.start()
    for s in range(SLOTS):
        for c in gu_copies(s, s):
            c.start()

    barrier = pltpu.get_barrier_semaphore()
    for peer in (partner, across):
        pl.semaphore_signal(barrier, inc=1, device_id=peer, device_id_type=MESH)
    pl.semaphore_wait(barrier, 2)

    x_copy.wait()

    def gu_step(i, carry):
        s = lax.rem(i, SLOTS)
        for c in gu_copies(i, s):
            c.wait()
        gate = jnp.dot(xv[...], w[s, 0], preferred_element_type=jnp.float32)
        up = jnp.dot(xv[...], w[s, 1], preferred_element_type=jnp.float32)
        h[:, pl.ds(pl.multiple_of(i * BN, BN), BN)] = (jax.nn.silu(gate) * up).astype(jnp.bfloat16)
        nxt = i + SLOTS

        @pl.when(nxt < NG)
        def _():
            for c in gu_copies(nxt, s):
                c.start()

        @pl.when(nxt >= NG)
        def _():
            for c in d_copies(nxt - NG, s):
                c.start()

        return carry

    lax.fori_loop(0, NG, gu_step, 0)

    def d_core(j):
        return pltpu.make_async_remote_copy(
            tb.at[j, theirs], rb.at[j], d_send.at[j], d_recv.at[j], device_id=partner, device_id_type=MESH)

    def d_across(j):
        return pltpu.make_async_remote_copy(
            ub.at[j], xr.at[j], u_send.at[j], u_recv.at[j], device_id=across, device_id_type=MESH)

    def d_gather(j):
        part = y_ref.at[mine, pl.ds(j * DB, DB)]
        return pltpu.make_async_remote_copy(
            part, part, g_send.at[j], g_recv.at[j], device_id=partner, device_id_type=MESH)

    def reduce_and_cross(j):
        d_core(j).wait_recv()
        ub[j] = (tf[j % 2, mine, :] + rb[j].astype(jnp.float32)).astype(jnp.bfloat16)
        d_across(j).start()

    def finish(j):
        d_across(j).wait_recv()
        y_ref[mine, pl.ds(j * DB, DB)] = (
            ub[j].astype(jnp.float32) + xr[j].astype(jnp.float32)).astype(jnp.bfloat16)
        d_gather(j).start()

    for j in range(ND):
        s = (NG + j) % SLOTS
        for q, c in enumerate(d_copies(j, s)):
            c.wait()
            term = jnp.dot(h[...], w[s, q], preferred_element_type=jnp.float32)
            tf[j % 2, :, pl.ds(q * BN, BN)] = term
            tb[j, :, pl.ds(q * BN, BN)] = term.astype(jnp.bfloat16)
        d_core(j).start()
        if j >= LAG_X:
            reduce_and_cross(j - LAG_X)
        if j >= LAG_Y:
            finish(j - LAG_Y)
    for j in range(ND - LAG_X, ND):
        reduce_and_cross(j)
    for j in range(ND - LAG_Y, ND):
        finish(j)
    for j in range(ND):
        d_core(j).wait_send()
        d_across(j).wait_send()
        d_gather(j).wait_send()
        d_gather(j).wait_recv()


def mlp(x, w_gate, w_up, w_down):
    bf = jnp.bfloat16
    dma = pltpu.SemaphoreType.DMA
    return pl.pallas_call(
        kernel,
        name="mlp",
        out_shape=jax.ShapeDtypeStruct((ROWS, D), bf),
        in_specs=[pl.BlockSpec(memory_space=pl.ANY)] * 4,
        out_specs=pl.BlockSpec(memory_space=pltpu.VMEM),
        scratch_shapes=[
            pltpu.VMEM((ROWS, D), bf),
            pltpu.VMEM((ROWS, F), bf),
            pltpu.VMEM((SLOTS, 2, D, BN), bf),
            pltpu.VMEM((ND, ROWS, DB), bf),
            pltpu.VMEM((2, ROWS, DB), jnp.float32),
            pltpu.VMEM((ND, HALF, DB), bf),
            pltpu.VMEM((ND, HALF, DB), bf),
            pltpu.VMEM((ND, HALF, DB), bf),
            dma, dma((SLOTS, 2)),
            dma((ND,)), dma((ND,)), dma((ND,)), dma((ND,)), dma((ND,)), dma((ND,)),
        ],
        compiler_params=pltpu.CompilerParams(
            collective_id=0, has_side_effects=True, vmem_limit_bytes=60 * 1024 * 1024),
    )(x, w_gate, w_up, w_down)


def solution(mesh):
    return jax.shard_map(
        mlp,
        mesh=mesh,
        in_specs=(P("dp", None), P(None, "tp"), P(None, "tp"), P("tp", None)),
        out_specs=P("dp", None),
        check_vma=False,
    )
```

time: 88.9 us -> 46 us (0.52)
  Pallas kernels: 0 us -> 43.5 us
  matrix products: 38 us -> 0 us
  waiting for transfers between devices: 33.8 us -> 0 us
  between operations: 13.4 us -> 0.01 us
  local copies, waits for them, and re-layouts: 3.51 us -> 2.29 us
    pallas_call x0 -> x1, Pallas kernels: none -> 43.5 us  [mlp(): pl.pallas_call(kernel, name='mlp', out_shape=jax.ShapeDtypeStruct((ROWS,...]
    dot_general x2 -> x0, matrix products: 38 us -> none  [the longest x1 25.1 us: step(): jnp.dot(hidden, w_down, preferred_element_type=jnp.float32)]
    psum x1 -> x0, waiting for transfers between devices: 33.8 us -> none  [step(): return lax.psum(term, 'tp')]
    unnamed x3 -> x1, local copies, waits for them, and re-layouts: 3.51 us -> 2.29 us
  transfers between devices with their start and end apart: 1 -> 0, of which waited for: 1 -> 0; matrix products, arithmetic and copies ran while one was open for 0% -> 0% of each run, Pallas kernels for 0% -> 0%
where the time goes in v1:
time: 46 us; the launch traced here: 45.8 us
  Pallas kernels  43.5 us (95%)
  local copies, waits for them, and re-layouts  2.29 us (5%)
    pallas_call x1, Pallas kernels, mlp(): pl.pallas_call(kernel, name='mlp', out_shape=jax.ShapeDtypeStruct((ROWS,...  43.5 us
    unnamed x1, local copies, waits for them, and re-layouts  2.29 us

profile of v1, /device:TPU:0, one launch (start us, length us, event | category | flops | bytes accessed | tf_op | source)
XLA Modules:
  0.0 45.8 jit_solution(7636087443657291579)
XLA Ops:
  0.0 43.5 %mlp.1 = bf16[128,4096]{1,0:T(8,128)(2,1)} custom-call(bf16[128,4096]{1,0:T(8,128)(2,1)} %x_hbm.1, bf16[4096,4096]{1,0:T(8,128)(2,1)} %wg_hbm.1, bf16[4096,4096]{1,0:T(8,128)(2,1)} %wu_hbm.1, bf16[4096,4096]{1,0:T(8,128)(2,1)} %wd_hbm.1), custom_call_target="tpu_custom_call" | custom-call | tf_op jit(solution)/shard_map/mlp/pallas_call | solution.py:132
  43.5 2.3 %copy.6 = bf16[128,4096]{1,0:T(8,128)(2,1)} copy(bf16[128,4096]{1,0:T(8,128)(2,1)} %mlp.1) | data formatting | bytes 2097152

commit v2 on v0

v2 whole, which is shorter than its diff:
```python
import functools

import jax
import jax.numpy as jnp
from jax import lax
from jax.experimental import pallas as pl
from jax.experimental.pallas import tpu as pltpu
from jax.sharding import PartitionSpec as P

MESH = pl.DeviceIdType.MESH
F32 = jnp.float32
BF16 = jnp.bfloat16
ROWS = 128
HALF = ROWS // 2
D = 4096
F = 4096
FH = F // 2
KC = 512
NK = D // KC
XC = 256
NR = 6
NC = 4
NB = 256
DB = 512
ND = D // DB
LAG = 3


def kernel(x_hbm, wg_hbm, wu_hbm, wd_hbm, y_ref,
           xs, xo, wg, wu, wd, acc_s, acc_o, h_s, h_o,
           tb_o, rb_o, uy, yr, tb_s, rb_s, ux, xr,
           x_sem, g_sem, u_sem, w_sem,
           yx_send, yx_recv, xx_send, xx_recv, dx_send, dx_recv,
           do_send, do_recv, uy_send, uy_recv, ds_send, ds_recv,
           ux_send, ux_recv, gy_send, gy_recv):
    grp = lax.axis_index("dp")
    tp = lax.axis_index("tp")
    core = lax.rem(tp, 2)
    chip = tp // 2
    partner = {"tp": 2 * chip + (1 - core)}
    xpeer = {"tp": 2 * (1 - chip) + core}
    ypeer = {"dp": 1 - grp}
    mine = pl.ds(pl.multiple_of(core * HALF, HALF), HALF)
    theirs = pl.ds(pl.multiple_of((1 - core) * HALF, HALF), HALF)
    units = pl.ds(pl.multiple_of(grp * FH, FH), FH)

    x_copy = pltpu.make_async_copy(x_hbm, xs, x_sem)

    def w_copies(k):
        rows = pl.ds(k * KC, KC)
        return (pltpu.make_async_copy(wg_hbm.at[rows, units], wg.at[k], g_sem.at[k]),
                pltpu.make_async_copy(wu_hbm.at[rows, units], wu.at[k], u_sem.at[k]))

    def wd_copy(j):
        return pltpu.make_async_copy(wd_hbm.at[units, pl.ds(j * DB, DB)], wd.at[j], w_sem.at[j])

    def push(src, dst, send, recv, peer):
        return pltpu.make_async_remote_copy(src, dst, send, recv, device_id=peer, device_id_type=MESH)

    def relay_k(i, c):
        return 2 * (i // 2) + c

    def relay_cols(i, c):
        return pl.ds(pl.multiple_of(relay_k(i, c) * KC + (i % 2) * XC, XC), XC)

    def y_cols(i):
        if i < NR:
            return relay_cols(i, chip)
        return pl.ds(2 * NR * XC + (i - NR) * XC, XC)

    def y_x(i):
        c = y_cols(i)
        return push(xs.at[mine, c], xo.at[mine, c], yx_send.at[i], yx_recv.at[i], ypeer)

    def x_x(i, c):
        c = relay_cols(i, c)
        return push(xo.at[mine, c], xo.at[mine, c], xx_send.at[i], xx_recv.at[i], xpeer)

    def d_x(i):
        c = y_cols(i) if i < NR + NC else relay_cols(i - NR - NC, 1 - chip)
        return push(xo.at[mine, c], xo.at[mine, c], dx_send.at[i], dx_recv.at[i], partner)

    def on_y(i):
        y_x(i).wait_recv()
        if i < NR:
            x_x(i, chip).start()
        d_x(i).start()

    def on_x(i):
        x_x(i, 1 - chip).wait_recv()
        d_x(NR + NC + i).start()

    x_copy.start()
    for k in range(NK):
        for c in w_copies(k):
            c.start()
    for j in range(ND):
        wd_copy(j).start()

    barrier = pltpu.get_barrier_semaphore()
    for peer in (partner, xpeer, ypeer):
        pl.semaphore_signal(barrier, inc=1, device_id=peer, device_id_type=MESH)
    pl.semaphore_wait(barrier, 3)

    x_copy.wait()
    for i in range(NR + NC):
        y_x(i).start()

    def gate_up(xref, acc, k, first=False, h=None):
        cols = pl.ds(k * KC if isinstance(k, int) else pl.multiple_of(k * KC, KC), KC)
        for n in range(0, FH, NB):
            nn = pl.ds(n, NB)
            g = jnp.dot(xref[:, cols], wg[k, :, nn], preferred_element_type=F32)
            u = jnp.dot(xref[:, cols], wu[k, :, nn], preferred_element_type=F32)
            if not first:
                g = acc[0, :, nn] + g
                u = acc[1, :, nn] + u
            if h is None:
                acc[0, :, nn] = g
                acc[1, :, nn] = u
            else:
                h[:, nn] = (jax.nn.silu(g) * u).astype(BF16)

    def own(k):
        for c in w_copies(k):
            c.wait()
        gate_up(xs, acc_s, k, first=k == 0, h=h_s if k == NK - 1 else None)

    def oth_y(r, first=False):
        for i in (2 * r, 2 * r + 1):
            d_x(i).wait_recv()
        gate_up(xo, acc_o, relay_k(2 * r, chip), first=first)

    def oth_x(r):
        for i in (2 * r, 2 * r + 1):
            d_x(NR + NC + i).wait_recv()
        gate_up(xo, acc_o, relay_k(2 * r, 1 - chip))

    def oth_c(r, last=False):
        for i in (2 * r, 2 * r + 1):
            d_x(NR + i).wait_recv()
        gate_up(xo, acc_o, NR + r, h=h_o if last else None)

    def wait_w(k):
        for c in w_copies(k):
            c.wait()

    own(0)
    own(1)
    on_y(0)
    own(2)
    on_y(1)
    on_y(2)
    own(3)
    on_y(3)
    oth_y(0, first=True)
    on_y(4)
    on_x(0)
    own(4)
    on_y(5)
    on_x(1)
    oth_y(1)
    on_y(6)
    on_x(2)
    own(5)
    on_y(7)
    oth_y(2)
    on_x(3)
    on_y(8)
    oth_x(0)
    on_x(4)
    on_y(9)
    on_x(5)
    wait_w(6)
    oth_c(0)
    oth_x(1)
    oth_x(2)
    wait_w(7)
    oth_c(1, last=True)

    def cols_of(j):
        return (j * DB) // FH, pl.ds((j * DB) % FH, DB)

    def term(h, acc, tb, j):
        q, cc = cols_of(j)
        acc[q, :, cc] = jnp.dot(h[...], wd[j], preferred_element_type=F32)
        tb[j] = acc[q, theirs, cc].astype(BF16)

    def core_o(j):
        return push(tb_o.at[j], rb_o.at[j], do_send.at[j], do_recv.at[j], partner)

    def core_s(j):
        return push(tb_s.at[j], rb_s.at[j], ds_send.at[j], ds_recv.at[j], partner)

    def over_y(j):
        return push(uy.at[j], yr.at[j], uy_send.at[j], uy_recv.at[j], ypeer)

    def over_x(j):
        return push(ux.at[j], xr.at[j], ux_send.at[j], ux_recv.at[j], xpeer)

    def gather(j):
        part = y_ref.at[mine, pl.ds(j * DB, DB)]
        return push(part, part, gy_send.at[j], gy_recv.at[j], partner)

    def send_y(j):
        q, cc = cols_of(j)
        core_o(j).wait_recv()
        uy[j] = (acc_o[q, mine, cc] + rb_o[j].astype(F32)).astype(BF16)
        over_y(j).start()

    def send_x(j):
        q, cc = cols_of(j)
        core_s(j).wait_recv()
        over_y(j).wait_recv()
        ux[j] = (acc_s[q, mine, cc] + rb_s[j].astype(F32) + yr[j].astype(F32)).astype(BF16)
        over_x(j).start()

    def finish(j):
        over_x(j).wait_recv()
        y_ref[mine, pl.ds(j * DB, DB)] = (ux[j].astype(F32) + xr[j].astype(F32)).astype(BF16)
        gather(j).start()

    def cross(j):
        send_x(j)
        if j >= LAG:
            finish(j - LAG)

    for j in range(ND):
        wd_copy(j).wait()
        term(h_o, acc_o, tb_o, j)
        core_o(j).start()
        if j >= 2:
            send_y(j - 2)
    gate_up(xs, acc_s, 6)
    send_y(ND - 2)
    send_y(ND - 1)
    gate_up(xs, acc_s, 7, h=h_s)
    for j in range(ND):
        term(h_s, acc_s, tb_s, j)
        core_s(j).start()
        if j >= LAG:
            cross(j - LAG)
    for j in range(ND - LAG, ND):
        cross(j)
    for j in range(ND - LAG, ND):
        finish(j)
    for i in range(NR + NC):
        y_x(i).wait_send()
        d_x(i).wait_send()
    for i in range(NR):
        x_x(i, chip).wait_send()
        d_x(NR + NC + i).wait_send()
    for j in range(ND):
        core_o(j).wait_send()
        core_s(j).wait_send()
        over_y(j).wait_send()
        over_x(j).wait_send()
        gather(j).wait_send()
        gather(j).wait_recv()


def mlp(x, w_gate, w_up, w_down):
    dma = pltpu.SemaphoreType.DMA
    part = pltpu.VMEM((ND, HALF, DB), BF16)
    return pl.pallas_call(
        kernel,
        name="mlp",
        out_shape=jax.ShapeDtypeStruct((ROWS, D), BF16),
        in_specs=[pl.BlockSpec(memory_space=pl.ANY)] * 4,
        out_specs=pl.BlockSpec(memory_space=pltpu.VMEM),
        scratch_shapes=[
            pltpu.VMEM((ROWS, D), BF16),
            pltpu.VMEM((ROWS, D), BF16),
            pltpu.VMEM((NK, KC, FH), BF16),
            pltpu.VMEM((NK, KC, FH), BF16),
            pltpu.VMEM((ND, FH, DB), BF16),
            pltpu.VMEM((2, ROWS, FH), F32),
            pltpu.VMEM((2, ROWS, FH), F32),
            pltpu.VMEM((ROWS, FH), BF16),
            pltpu.VMEM((ROWS, FH), BF16),
            part, part, part, part, part, part, part, part,
            dma, dma((NK,)), dma((NK,)), dma((ND,)),
            dma((NR + NC,)), dma((NR + NC,)), dma((NR,)), dma((NR,)),
            dma((2 * NR + NC,)), dma((2 * NR + NC,)),
            dma((ND,)), dma((ND,)), dma((ND,)), dma((ND,)), dma((ND,)), dma((ND,)),
            dma((ND,)), dma((ND,)), dma((ND,)), dma((ND,)),
        ],
        compiler_params=pltpu.CompilerParams(
            collective_id=0, has_side_effects=True, vmem_limit_bytes=67043328),
    )(x, w_gate, w_up, w_down)


def solution(mesh):
    return jax.shard_map(
        mlp,
        mesh=mesh,
        in_specs=(P("dp", None), P(None, "tp"), P(None, "tp"), P("tp", None)),
        out_specs=P("dp", None),
        check_vma=False,
    )
```

time: 88.9 us -> 56.5 us (0.64)
  Pallas kernels: 0 us -> 54.1 us
  matrix products: 38 us -> 0 us
  waiting for transfers between devices: 33.8 us -> 0 us
  between operations: 13.4 us -> 0.01 us
  local copies, waits for them, and re-layouts: 3.51 us -> 2.29 us
    pallas_call x0 -> x1, Pallas kernels: none -> 54.1 us  [mlp(): pl.pallas_call(kernel, name='mlp', out_shape=jax.ShapeDtypeStruct((ROWS,...]
    dot_general x2 -> x0, matrix products: 38 us -> none  [the longest x1 25.1 us: step(): jnp.dot(hidden, w_down, preferred_element_type=jnp.float32)]
    psum x1 -> x0, waiting for transfers between devices: 33.8 us -> none  [step(): return lax.psum(term, 'tp')]
    unnamed x3 -> x1, local copies, waits for them, and re-layouts: 3.51 us -> 2.29 us
  transfers between devices with their start and end apart: 1 -> 0, of which waited for: 1 -> 0; matrix products, arithmetic and copies ran while one was open for 0% -> 0% of each run, Pallas kernels for 0% -> 0%
where the time goes in v2:
time: 56.5 us; the launch traced here: 56.4 us
  Pallas kernels  54.1 us (96%)
  local copies, waits for them, and re-layouts  2.29 us (4%)
    pallas_call x1, Pallas kernels, mlp(): pl.pallas_call(kernel, name='mlp', out_shape=jax.ShapeDtypeStruct((ROWS,...  54.1 us
    unnamed x1, local copies, waits for them, and re-layouts  2.29 us

profile of v2, /device:TPU:0, one launch (start us, length us, event | category | flops | bytes accessed | tf_op | source)
XLA Modules:
  0.0 56.4 jit_solution(5568859504944076082)
XLA Ops:
  0.0 54.1 %mlp.1 = bf16[128,4096]{1,0:T(8,128)(2,1)} custom-call(bf16[128,4096]{1,0:T(8,128)(2,1)} %x_hbm.1, bf16[4096,4096]{1,0:T(8,128)(2,1)} %wg_hbm.1, bf16[4096,4096]{1,0:T(8,128)(2,1)} %wu_hbm.1, bf16[4096,4096]{1,0:T(8,128)(2,1)} %wd_hbm.1), custom_call_target="tpu_custom_call" | custom-call | tf_op jit(solution)/shard_map/mlp/pallas_call | solution.py:265
  54.1 2.3 %copy.6 = bf16[128,4096]{1,0:T(8,128)(2,1)} copy(bf16[128,4096]{1,0:T(8,128)(2,1)} %mlp.1) | data formatting | bytes 2097152

commit v3 on v2

--- a/solution.py
+++ b/solution.py
@@ -24,6 +24,7 @@
 DB = 512
 ND = D // DB
 LAG = 3
+DEPTH = 2
 
 
 def kernel(x_hbm, wg_hbm, wu_hbm, wd_hbm, y_ref,
@@ -91,11 +92,13 @@
         d_x(NR + NC + i).start()
 
     x_copy.start()
-    for k in range(NK):
-        for c in w_copies(k):
-            c.start()
-    for j in range(ND):
-        wd_copy(j).start()
+    def more(n):
+        for _ in range(n):
+            if queue:
+                queue.pop(0).start()
+
+    queue = [c for k in range(NK) for c in w_copies(k)] + [wd_copy(j) for j in range(ND)]
+    more(2 * DEPTH)
 
     barrier = pltpu.get_barrier_semaphore()
     for peer in (partner, xpeer, ypeer):
@@ -122,8 +125,7 @@
                 h[:, nn] = (jax.nn.silu(g) * u).astype(BF16)
 
     def own(k):
-        for c in w_copies(k):
-            c.wait()
+        wait_w(k)
         gate_up(xs, acc_s, k, first=k == 0, h=h_s if k == NK - 1 else None)
 
     def oth_y(r, first=False):
@@ -144,6 +146,7 @@
     def wait_w(k):
         for c in w_copies(k):
             c.wait()
+            more(1)
 
     own(0)
     own(1)
@@ -227,6 +230,7 @@
 
     for j in range(ND):
         wd_copy(j).wait()
+        more(1)
         term(h_o, acc_o, tb_o, j)
         core_o(j).start()
         if j >= 2:

time: 56.5 us -> 44.6 us (0.79)
  Pallas kernels: 54.1 us -> 42.2 us
    pallas_call x1, Pallas kernels: 54.1 us -> 42.2 us  [mlp(): pl.pallas_call(kernel, name='mlp', out_shape=jax.ShapeDtypeStruct((ROWS,...]
where the time goes in v3:
time: 44.6 us; the launch traced here: 44.5 us
  Pallas kernels  42.2 us (95%)
  local copies, waits for them, and re-layouts  2.29 us (5%)
    pallas_call x1, Pallas kernels, mlp(): pl.pallas_call(kernel, name='mlp', out_shape=jax.ShapeDtypeStruct((ROWS,...  42.2 us
    unnamed x1, local copies, waits for them, and re-layouts  2.29 us

profile of v3, /device:TPU:0, one launch (start us, length us, event | category | flops | bytes accessed | tf_op | source)
XLA Modules:
  0.0 44.5 jit_solution(4161652856259978821)
XLA Ops:
  0.0 42.2 %mlp.1 = bf16[128,4096]{1,0:T(8,128)(2,1)} custom-call(bf16[128,4096]{1,0:T(8,128)(2,1)} %x_hbm.1, bf16[4096,4096]{1,0:T(8,128)(2,1)} %wg_hbm.1, bf16[4096,4096]{1,0:T(8,128)(2,1)} %wu_hbm.1, bf16[4096,4096]{1,0:T(8,128)(2,1)} %wd_hbm.1), custom_call_target="tpu_custom_call" | custom-call | tf_op jit(solution)/shard_map/mlp/pallas_call | solution.py:269
  42.2 2.3 %copy.6 = bf16[128,4096]{1,0:T(8,128)(2,1)} copy(bf16[128,4096]{1,0:T(8,128)(2,1)} %mlp.1) | data formatting | bytes 2097152

commit v4 on v3

--- a/solution.py
+++ b/solution.py
@@ -24,7 +24,8 @@
 DB = 512
 ND = D // DB
 LAG = 3
-DEPTH = 2
+KP = 128
+FP = 512
 
 
 def kernel(x_hbm, wg_hbm, wu_hbm, wd_hbm, y_ref,
@@ -52,8 +53,20 @@
         return (pltpu.make_async_copy(wg_hbm.at[rows, units], wg.at[k], g_sem.at[k]),
                 pltpu.make_async_copy(wu_hbm.at[rows, units], wu.at[k], u_sem.at[k]))
 
+    def w_pieces(k):
+        for p in range(0, KC, KP):
+            rows = pl.ds(k * KC + p, KP)
+            yield pltpu.make_async_copy(wg_hbm.at[rows, units], wg.at[k, pl.ds(p, KP)], g_sem.at[k])
+            yield pltpu.make_async_copy(wu_hbm.at[rows, units], wu.at[k, pl.ds(p, KP)], u_sem.at[k])
+
     def wd_copy(j):
         return pltpu.make_async_copy(wd_hbm.at[units, pl.ds(j * DB, DB)], wd.at[j], w_sem.at[j])
+
+    def wd_pieces(j):
+        for p in range(0, FH, FP):
+            rows = pl.ds(pl.multiple_of(grp * FH + p, FP), FP)
+            yield pltpu.make_async_copy(
+                wd_hbm.at[rows, pl.ds(j * DB, DB)], wd.at[j, pl.ds(p, FP)], w_sem.at[j])
 
     def push(src, dst, send, recv, peer):
         return pltpu.make_async_remote_copy(src, dst, send, recv, device_id=peer, device_id_type=MESH)
@@ -97,8 +110,8 @@
             if queue:
                 queue.pop(0).start()
 
-    queue = [c for k in range(NK) for c in w_copies(k)] + [wd_copy(j) for j in range(ND)]
-    more(2 * DEPTH)
+    queue = [c for k in range(NK) for c in w_pieces(k)] + [c for j in range(ND) for c in wd_pieces(j)]
+    more(8)
 
     barrier = pltpu.get_barrier_semaphore()
     for peer in (partner, xpeer, ypeer):
@@ -108,10 +121,13 @@
     x_copy.wait()
     for i in range(NR + NC):
         y_x(i).start()
-
-    def gate_up(xref, acc, k, first=False, h=None):
+    more(8)
+
+    def gate_up(xref, acc, k, first=False, h=None, pieces=4):
         cols = pl.ds(k * KC if isinstance(k, int) else pl.multiple_of(k * KC, KC), KC)
         for n in range(0, FH, NB):
+            if (n // NB) % (8 // pieces) == 0:
+                more(1)
             nn = pl.ds(n, NB)
             g = jnp.dot(xref[:, cols], wg[k, :, nn], preferred_element_type=F32)
             u = jnp.dot(xref[:, cols], wu[k, :, nn], preferred_element_type=F32)
@@ -126,7 +142,7 @@
 
     def own(k):
         wait_w(k)
-        gate_up(xs, acc_s, k, first=k == 0, h=h_s if k == NK - 1 else None)
+        gate_up(xs, acc_s, k, first=k == 0, pieces=8 if k < 4 else 4)
 
     def oth_y(r, first=False):
         for i in (2 * r, 2 * r + 1):
@@ -146,7 +162,6 @@
     def wait_w(k):
         for c in w_copies(k):
             c.wait()
-            more(1)
 
     own(0)
     own(1)
@@ -230,7 +245,7 @@
 
     for j in range(ND):
         wd_copy(j).wait()
-        more(1)
+        more(4)
         term(h_o, acc_o, tb_o, j)
         core_o(j).start()
         if j >= 2:

time: 44.6 us -> 44.6 us (level)
  no operation moved by 1% of the time
where the time goes in v4:
time: 44.6 us; the launch traced here: 44.5 us
  Pallas kernels  42.2 us (95%)
  local copies, waits for them, and re-layouts  2.29 us (5%)
    pallas_call x1, Pallas kernels, mlp(): pl.pallas_call(kernel, name='mlp', out_shape=jax.ShapeDtypeStruct((ROWS,...  42.2 us
    unnamed x1, local copies, waits for them, and re-layouts  2.29 us

profile of v4, /device:TPU:0, one launch (start us, length us, event | category | flops | bytes accessed | tf_op | source)
XLA Modules:
  0.0 44.5 jit_solution(11073585065387198205)
XLA Ops:
  0.0 42.2 %mlp.1 = bf16[128,4096]{1,0:T(8,128)(2,1)} custom-call(bf16[128,4096]{1,0:T(8,128)(2,1)} %x_hbm.1, bf16[4096,4096]{1,0:T(8,128)(2,1)} %wg_hbm.1, bf16[4096,4096]{1,0:T(8,128)(2,1)} %wu_hbm.1, bf16[4096,4096]{1,0:T(8,128)(2,1)} %wd_hbm.1), custom_call_target="tpu_custom_call" | custom-call | tf_op jit(solution)/shard_map/mlp/pallas_call | solution.py:284
  42.2 2.3 %copy.6 = bf16[128,4096]{1,0:T(8,128)(2,1)} copy(bf16[128,4096]{1,0:T(8,128)(2,1)} %mlp.1) | data formatting | bytes 2097152

commit v5 on v4

v5 whole, which is shorter than its diff:
```python
import jax
import jax.numpy as jnp
from jax import lax
from jax.experimental import pallas as pl
from jax.experimental.pallas import tpu as pltpu
from jax.sharding import PartitionSpec as P

MESH = pl.DeviceIdType.MESH
F32 = jnp.float32
BF16 = jnp.bfloat16
ROWS = 128
HALF = ROWS // 2
D = 4096
F = 4096
FH = F // 2
KC = 512
NK = D // KC
XC = 256
NR = 6
NC = 4
NB = 256
DB = 512
ND = D // DB
KP = 128
FP = 512
XP = 16
PREFILL = 2
START = 4
WIDTHS = (256, 256, 512, 512, 512, 512, 512, 512, 256, 256)
NT = len(WIDTHS)
OFFS = tuple(sum(WIDTHS[:j]) for j in range(NT))

SCHEDULE = (
    ('i',4), ('i',1), ('i',1), ('i',1), ('i',1), ('i',1), ('i',1), ('i',1), ('i',1), ('i',1), ('i',1), ('i',1),
    ('y',0), ('i',1), ('i',1), ('s',0,0,(0,0,0,0)), ('s',0,1,(0,0,0,0)), ('y',1), ('i',4), ('i',1), ('i',1),
    ('i',1), ('y',2), ('i',1), ('s',1,0,(0,0,0,0)), ('s',1,1,(0,0,0,0)), ('y',3), ('o','y0',(0,0,1,0,1,0,0,1)),
    ('x',0), ('i',4), ('i',1), ('y',4), ('i',1), ('i',1), ('s',2,0,(0,0,0,0)), ('x',1), ('s',2,1,(0,0,0,0)),
    ('y',5), ('o','y1',(0,0,0,1,0,1,0,1)), ('y',6), ('x',2), ('s',3,0,(0,1,0,1)), ('o','x0',(0,0,1,0,1,0,1,0)),
    ('y',7), ('x',3), ('s',3,1,(1,0,1,0)), ('x',4), ('s',4,0,(1,0,0,1)), ('y',8), ('s',4,1,(0,1,0,1)),
    ('o','y2',(0,1,0,1,0,0,1,0)), ('y',9), ('x',5), ('o','x1',(1,0,1,0,1,0,1,0)), ('s',5,0,(0,1,0,1)),
    ('o','c0',(0,1,0,1,0,1,0,0)), ('o','x2',(1,0,1,0,1,0,0,1)), ('o','c1',(0,1,0,1,0,1,0,0)),
    ('s',5,1,(1,0,1,0)), ('t',0,(1,)), ('t',1,(1,)), ('t',2,(1,)), ('s',6,0,(2,0,1,0)), ('s',6,1,(1,0,1,0)),
    ('e',0), ('t',3,(0,)), ('e',1), ('s',7,0,(1,1,0,1)), ('e',2), ('s',7,1,(0,1,0,1)), ('t',4,(0,)),
    ('t',5,(1,)), ('e',3), ('S',0,(2,)), ('S',1,(2,)), ('S',2,(1,)), ('t',6,(1,)), ('e',4), ('S',3,(0,)),
    ('e',5), ('S',4,(0,)), ('c',0), ('t',7,(0,)), ('c',1), ('S',5,(0,)), ('e',6), ('t',8,(0,)), ('t',9,(0,)),
    ('S',6,(0,)), ('S',7,(0,)), ('e',7), ('c',2), ('S',8,(0,)), ('S',9,(0,)), ('e',8), ('e',9), ('f',0),
    ('c',3), ('f',1), ('c',4), ('f',2), ('c',5), ('f',3), ('c',6), ('f',4), ('c',7), ('f',5), ('c',8), ('c',9),
    ('f',6), ('f',7), ('f',8), ('f',9),
)


def kernel(x_hbm, wg_hbm, wu_hbm, wd_hbm, y_ref,
           xs, xo, wg, wu, wd, acc_s, acc_o, h_s, h_o,
           tb_o, rb_o, uy, yr, tb_s, rb_s, ux, xr,
           x_sem, g_sem, u_sem, w_sem,
           yx_send, yx_recv, xx_send, xx_recv, dx_send, dx_recv,
           do_send, do_recv, uy_send, uy_recv, ds_send, ds_recv,
           ux_send, ux_recv, gy_send, gy_recv):
    grp = lax.axis_index("dp")
    tp = lax.axis_index("tp")
    core = lax.rem(tp, 2)
    chip = tp // 2
    partner = {"tp": 2 * chip + (1 - core)}
    xpeer = {"tp": 2 * (1 - chip) + core}
    ypeer = {"dp": 1 - grp}
    mine = pl.ds(pl.multiple_of(core * HALF, HALF), HALF)
    theirs = pl.ds(pl.multiple_of((1 - core) * HALF, HALF), HALF)
    units = pl.ds(pl.multiple_of(grp * FH, FH), FH)

    barrier = pltpu.get_barrier_semaphore()
    for peer in (partner, xpeer, ypeer):
        pl.semaphore_signal(barrier, inc=1, device_id=peer, device_id_type=MESH)

    for p in range(0, HALF, XP):
        rows = pl.ds(pl.multiple_of(core * HALF + p, XP), XP)
        pltpu.make_async_copy(x_hbm.at[rows], xs.at[rows], x_sem.at[0]).start()
    x_mine = pltpu.make_async_copy(x_hbm.at[mine], xs.at[mine], x_sem.at[0])
    x_theirs = pltpu.make_async_copy(x_hbm.at[theirs], xs.at[theirs], x_sem.at[1])

    def w_copies(k):
        rows = pl.ds(k * KC, KC)
        return (pltpu.make_async_copy(wg_hbm.at[rows, units], wg.at[k], g_sem.at[k]),
                pltpu.make_async_copy(wu_hbm.at[rows, units], wu.at[k], u_sem.at[k]))

    def w_pieces(k):
        for p in range(0, KC, KP):
            rows = pl.ds(k * KC + p, KP)
            yield pltpu.make_async_copy(wg_hbm.at[rows, units], wg.at[k, pl.ds(p, KP)], g_sem.at[k])
            yield pltpu.make_async_copy(wu_hbm.at[rows, units], wu.at[k, pl.ds(p, KP)], u_sem.at[k])

    def wd_copy(j):
        return pltpu.make_async_copy(wd_hbm.at[units, pl.ds(j * DB, DB)], wd.at[j], w_sem.at[j])

    def wd_pieces(j):
        for p in range(0, FH, FP):
            rows = pl.ds(pl.multiple_of(grp * FH + p, FP), FP)
            yield pltpu.make_async_copy(
                wd_hbm.at[rows, pl.ds(j * DB, DB)], wd.at[j, pl.ds(p, FP)], w_sem.at[j])

    queue = [c for k in range(NK) for c in w_pieces(k)] + [c for j in range(ND) for c in wd_pieces(j)]

    def more(n):
        for _ in range(n):
            if queue:
                queue.pop(0).start()

    def push(src, dst, send, recv, peer):
        return pltpu.make_async_remote_copy(src, dst, send, recv, device_id=peer, device_id_type=MESH)

    def relay_k(i, c):
        return 2 * (i // 2) + c

    def relay_cols(i, c):
        return pl.ds(pl.multiple_of(relay_k(i, c) * KC + (i % 2) * XC, XC), XC)

    def y_cols(i):
        if i < NR:
            return relay_cols(i, chip)
        return pl.ds(2 * NR * XC + (i - NR) * XC, XC)

    def y_x(i):
        c = y_cols(i)
        return push(xs.at[mine, c], xo.at[mine, c], yx_send.at[i], yx_recv.at[i], ypeer)

    def x_x(i, c):
        c = relay_cols(i, c)
        return push(xo.at[mine, c], xo.at[mine, c], xx_send.at[i], xx_recv.at[i], xpeer)

    def d_x(i):
        c = y_cols(i) if i < NR + NC else relay_cols(i - NR - NC, 1 - chip)
        return push(xo.at[mine, c], xo.at[mine, c], dx_send.at[i], dx_recv.at[i], partner)

    def on_y(i):
        y_x(i).wait_recv()
        if i < NR:
            x_x(i, chip).start()
        d_x(i).start()

    def on_x(i):
        x_x(i, 1 - chip).wait_recv()
        d_x(NR + NC + i).start()

    waited = set()

    def wait_w(*ks):
        for k in ks:
            if k not in waited:
                waited.add(k)
                for c in w_copies(k):
                    c.wait()

    def wait_wd(j):
        if ("d", j) not in waited:
            waited.add(("d", j))
            wd_copy(j).wait()

    def gate_up(xref, acc, k, lo, hi, counts, first, h):
        cols = pl.ds(k * KC if isinstance(k, int) else pl.multiple_of(k * KC, KC), KC)
        for n in range(lo, hi, NB):
            more(counts[(n - lo) // NB])
            nn = pl.ds(n, NB)
            g = jnp.dot(xref[:, cols], wg[k, :, nn], preferred_element_type=F32)
            u = jnp.dot(xref[:, cols], wu[k, :, nn], preferred_element_type=F32)
            if not first:
                g = acc[0, :, nn] + g
                u = acc[1, :, nn] + u
            if h is None:
                acc[0, :, nn] = g
                acc[1, :, nn] = u
            else:
                h[:, nn] = (jax.nn.silu(g) * u).astype(BF16)

    def own(k, half, counts):
        wait_w(k)
        if "x" not in waited:
            waited.add("x")
            x_theirs.wait()
        lo = half * (FH // 2)
        gate_up(xs, acc_s, k, lo, lo + FH // 2, counts, k == 0, h_s if k == NK - 1 else None)

    slots = [t[1] for t in SCHEDULE if t[0] == "o"]

    def other(slot, counts):
        kind, r = slot[0], int(slot[1])
        if kind == "c":
            wait_w(NR + r)
            k = NR + r
            ready = (NR + 2 * r, NR + 2 * r + 1)
        else:
            wait_w(2 * r, 2 * r + 1)
            k = relay_k(2 * r, chip if kind == "y" else 1 - chip)
            base = 0 if kind == "y" else NR + NC
            ready = (base + 2 * r, base + 2 * r + 1)
        for i in ready:
            d_x(i).wait_recv()
        gate_up(xo, acc_o, k, 0, FH, counts, slot == slots[0], h_o if slot == slots[-1] else None)

    def block(j):
        return pl.ds(OFFS[j], WIDTHS[j])

    def term(h, acc, tb, j, counts):
        o, w = OFFS[j], WIDTHS[j]
        wait_wd(o // DB)
        more(counts[0])
        acc[o // FH, :, pl.ds(o % FH, w)] = jnp.dot(
            h[...], wd[o // DB, :, pl.ds(o % DB, w)], preferred_element_type=F32)
        tb[:, block(j)] = acc[o // FH, theirs, pl.ds(o % FH, w)].astype(BF16)

    def part(acc, j):
        o, w = OFFS[j], WIDTHS[j]
        return acc[o // FH, mine, pl.ds(o % FH, w)]

    def core_o(j):
        return push(tb_o.at[:, block(j)], rb_o.at[:, block(j)], do_send.at[j], do_recv.at[j], partner)

    def core_s(j):
        return push(tb_s.at[:, block(j)], rb_s.at[:, block(j)], ds_send.at[j], ds_recv.at[j], partner)

    def over_y(j):
        return push(uy.at[:, block(j)], yr.at[:, block(j)], uy_send.at[j], uy_recv.at[j], ypeer)

    def over_x(j):
        return push(ux.at[:, block(j)], xr.at[:, block(j)], ux_send.at[j], ux_recv.at[j], xpeer)

    def gather(j):
        rows = y_ref.at[mine, block(j)]
        return push(rows, rows, gy_send.at[j], gy_recv.at[j], partner)

    def send_y(j):
        core_o(j).wait_recv()
        uy[:, block(j)] = (part(acc_o, j) + rb_o[:, block(j)].astype(F32)).astype(BF16)
        over_y(j).start()

    def send_x(j):
        core_s(j).wait_recv()
        over_y(j).wait_recv()
        ux[:, block(j)] = (part(acc_s, j) + rb_s[:, block(j)].astype(F32)
                           + yr[:, block(j)].astype(F32)).astype(BF16)
        over_x(j).start()

    def finish(j):
        over_x(j).wait_recv()
        y_ref[mine, block(j)] = (ux[:, block(j)].astype(F32) + xr[:, block(j)].astype(F32)).astype(BF16)
        gather(j).start()

    more(PREFILL)
    pl.semaphore_wait(barrier, 3)
    x_mine.wait()
    for i in range(NR + NC):
        y_x(i).start()
    x_theirs.start()
    more(START)

    for kind, i, *rest in SCHEDULE:
        if kind == "y":
            on_y(i)
        elif kind == "x":
            on_x(i)
        elif kind == "s":
            own(i, *rest)
        elif kind == "o":
            other(i, *rest)
        elif kind == "t":
            term(h_o, acc_o, tb_o, i, *rest)
            core_o(i).start()
        elif kind == "S":
            term(h_s, acc_s, tb_s, i, *rest)
            core_s(i).start()
        elif kind == "e":
            send_y(i)
        elif kind == "c":
            send_x(i)
        elif kind == "f":
            finish(i)
        else:
            more(i)

    for j in range(NT):
        gather(j).wait_recv()
    for i in range(NR + NC):
        y_x(i).wait_send()
        d_x(i).wait_send()
    for i in range(NR):
        x_x(i, chip).wait_send()
        d_x(NR + NC + i).wait_send()
    for j in range(NT):
        core_o(j).wait_send()
        core_s(j).wait_send()
        over_y(j).wait_send()
        over_x(j).wait_send()
        gather(j).wait_send()


def mlp(x, w_gate, w_up, w_down):
    dma = pltpu.SemaphoreType.DMA
    half = pltpu.VMEM((HALF, D), BF16)
    return pl.pallas_call(
        kernel,
        name="mlp",
        out_shape=jax.ShapeDtypeStruct((ROWS, D), BF16),
        in_specs=[pl.BlockSpec(memory_space=pl.ANY)] * 4,
        out_specs=pl.BlockSpec(memory_space=pltpu.VMEM),
        scratch_shapes=[
            pltpu.VMEM((ROWS, D), BF16),
            pltpu.VMEM((ROWS, D), BF16),
            pltpu.VMEM((NK, KC, FH), BF16),
            pltpu.VMEM((NK, KC, FH), BF16),
            pltpu.VMEM((ND, FH, DB), BF16),
            pltpu.VMEM((2, ROWS, FH), F32),
            pltpu.VMEM((2, ROWS, FH), F32),
            pltpu.VMEM((ROWS, FH), BF16),
            pltpu.VMEM((ROWS, FH), BF16),
            half, half, half, half, half, half, half, half,
            dma((2,)), dma((NK,)), dma((NK,)), dma((ND,)),
            dma((NR + NC,)), dma((NR + NC,)), dma((NR,)), dma((NR,)),
            dma((2 * NR + NC,)), dma((2 * NR + NC,)),
            dma((NT,)), dma((NT,)), dma((NT,)), dma((NT,)), dma((NT,)), dma((NT,)),
            dma((NT,)), dma((NT,)), dma((NT,)), dma((NT,)),
        ],
        compiler_params=pltpu.CompilerParams(
            collective_id=0, has_side_effects=True, vmem_limit_bytes=67043328),
    )(x, w_gate, w_up, w_down)


def solution(mesh):
    return jax.shard_map(
        mlp,
        mesh=mesh,
        in_specs=(P("dp", None), P(None, "tp"), P(None, "tp"), P("tp", None)),
        out_specs=P("dp", None),
        check_vma=False,
    )
```

time: 44.6 us -> 47.1 us (1.056)
  Pallas kernels: 42.2 us -> 44.7 us
    pallas_call x1, Pallas kernels: 42.2 us -> 44.7 us  [mlp(): pl.pallas_call(kernel, name='mlp', out_shape=jax.ShapeDtypeStruct((ROWS,...]
where the time goes in v5:
time: 47.1 us; the launch traced here: 47 us
  Pallas kernels  44.7 us (95%)
  local copies, waits for them, and re-layouts  2.29 us (5%)
    pallas_call x1, Pallas kernels, mlp(): pl.pallas_call(kernel, name='mlp', out_shape=jax.ShapeDtypeStruct((ROWS,...  44.7 us
    unnamed x1, local copies, waits for them, and re-layouts  2.29 us

profile of v5, /device:TPU:0, one launch (start us, length us, event | category | flops | bytes accessed | tf_op | source)
XLA Modules:
  0.0 47.0 jit_solution(7692016689913065328)
XLA Ops:
  0.0 44.7 %mlp.1 = bf16[128,4096]{1,0:T(8,128)(2,1)} custom-call(bf16[128,4096]{1,0:T(8,128)(2,1)} %x_hbm.1, bf16[4096,4096]{1,0:T(8,128)(2,1)} %wg_hbm.1, bf16[4096,4096]{1,0:T(8,128)(2,1)} %wu_hbm.1, bf16[4096,4096]{1,0:T(8,128)(2,1)} %wd_hbm.1), custom_call_target="tpu_custom_call" | custom-call | tf_op jit(solution)/shard_map/mlp/pallas_call | solution.py:297
  44.7 2.3 %copy.6 = bf16[128,4096]{1,0:T(8,128)(2,1)} copy(bf16[128,4096]{1,0:T(8,128)(2,1)} %mlp.1) | data formatting | bytes 2097152

commit v6 on v5

--- a/solution.py
+++ b/solution.py
@@ -21,38 +21,28 @@
 NB = 256
 DB = 512
 ND = D // DB
-KP = 128
-FP = 512
 XP = 16
-PREFILL = 2
-START = 4
 WIDTHS = (256, 256, 512, 512, 512, 512, 512, 512, 256, 256)
 NT = len(WIDTHS)
 OFFS = tuple(sum(WIDTHS[:j]) for j in range(NT))
 
 SCHEDULE = (
-    ('i',4), ('i',1), ('i',1), ('i',1), ('i',1), ('i',1), ('i',1), ('i',1), ('i',1), ('i',1), ('i',1), ('i',1),
-    ('y',0), ('i',1), ('i',1), ('s',0,0,(0,0,0,0)), ('s',0,1,(0,0,0,0)), ('y',1), ('i',4), ('i',1), ('i',1),
-    ('i',1), ('y',2), ('i',1), ('s',1,0,(0,0,0,0)), ('s',1,1,(0,0,0,0)), ('y',3), ('o','y0',(0,0,1,0,1,0,0,1)),
-    ('x',0), ('i',4), ('i',1), ('y',4), ('i',1), ('i',1), ('s',2,0,(0,0,0,0)), ('x',1), ('s',2,1,(0,0,0,0)),
-    ('y',5), ('o','y1',(0,0,0,1,0,1,0,1)), ('y',6), ('x',2), ('s',3,0,(0,1,0,1)), ('o','x0',(0,0,1,0,1,0,1,0)),
-    ('y',7), ('x',3), ('s',3,1,(1,0,1,0)), ('x',4), ('s',4,0,(1,0,0,1)), ('y',8), ('s',4,1,(0,1,0,1)),
-    ('o','y2',(0,1,0,1,0,0,1,0)), ('y',9), ('x',5), ('o','x1',(1,0,1,0,1,0,1,0)), ('s',5,0,(0,1,0,1)),
-    ('o','c0',(0,1,0,1,0,1,0,0)), ('o','x2',(1,0,1,0,1,0,0,1)), ('o','c1',(0,1,0,1,0,1,0,0)),
-    ('s',5,1,(1,0,1,0)), ('t',0,(1,)), ('t',1,(1,)), ('t',2,(1,)), ('s',6,0,(2,0,1,0)), ('s',6,1,(1,0,1,0)),
-    ('e',0), ('t',3,(0,)), ('e',1), ('s',7,0,(1,1,0,1)), ('e',2), ('s',7,1,(0,1,0,1)), ('t',4,(0,)),
-    ('t',5,(1,)), ('e',3), ('S',0,(2,)), ('S',1,(2,)), ('S',2,(1,)), ('t',6,(1,)), ('e',4), ('S',3,(0,)),
-    ('e',5), ('S',4,(0,)), ('c',0), ('t',7,(0,)), ('c',1), ('S',5,(0,)), ('e',6), ('t',8,(0,)), ('t',9,(0,)),
-    ('S',6,(0,)), ('S',7,(0,)), ('e',7), ('c',2), ('S',8,(0,)), ('S',9,(0,)), ('e',8), ('e',9), ('f',0),
-    ('c',3), ('f',1), ('c',4), ('f',2), ('c',5), ('f',3), ('c',6), ('f',4), ('c',7), ('f',5), ('c',8), ('c',9),
-    ('f',6), ('f',7), ('f',8), ('f',9),
+    ('s',0,0), ('s',0,1), ('y',0), ('s',1,0), ('s',1,1), ('y',1), ('y',2), ('s',2,0), ('s',2,1), ('y',3),
+    ('o','y0'), ('y',4), ('x',0), ('s',3,0), ('o','y1'), ('y',5), ('x',1), ('s',3,1), ('y',6), ('x',2),
+    ('s',4,0), ('s',4,1), ('y',7), ('x',3), ('o','x0'), ('y',8), ('x',4), ('o','y2'), ('y',9), ('x',5),
+    ('o','x1'), ('o','c0'), ('o','x2'), ('o','c1'), ('t',0), ('t',1), ('t',2), ('s',5,0), ('s',5,1), ('e',0),
+    ('e',1), ('s',6,0), ('t',3), ('e',2), ('s',6,1), ('s',7,0), ('s',7,1), ('t',4), ('e',3), ('S',0), ('S',1),
+    ('S',2), ('t',5), ('e',4), ('S',3), ('c',0), ('c',1), ('S',4), ('S',5), ('c',2), ('t',6), ('e',5), ('S',6),
+    ('t',7), ('S',7), ('c',3), ('t',8), ('e',6), ('f',0), ('S',8), ('t',9), ('e',7), ('S',9), ('f',1), ('c',4),
+    ('e',8), ('e',9), ('f',2), ('c',5), ('f',3), ('c',6), ('f',4), ('c',7), ('c',8), ('f',5), ('c',9), ('f',6),
+    ('f',7), ('f',8), ('f',9),
 )
 
 
 def kernel(x_hbm, wg_hbm, wu_hbm, wd_hbm, y_ref,
            xs, xo, wg, wu, wd, acc_s, acc_o, h_s, h_o,
            tb_o, rb_o, uy, yr, tb_s, rb_s, ux, xr,
-           x_sem, g_sem, u_sem, w_sem,
+           f_sem, x_sem, g_sem, u_sem, w_sem,
            yx_send, yx_recv, xx_send, xx_recv, dx_send, dx_recv,
            do_send, do_recv, uy_send, uy_recv, ds_send, ds_recv,
            ux_send, ux_recv, gy_send, gy_recv):
@@ -67,6 +57,10 @@
     theirs = pl.ds(pl.multiple_of((1 - core) * HALF, HALF), HALF)
     units = pl.ds(pl.multiple_of(grp * FH, FH), FH)
 
+    def fence():
+        pl.semaphore_signal(f_sem, 1)
+        pl.semaphore_wait(f_sem, 1)
+
     barrier = pltpu.get_barrier_semaphore()
     for peer in (partner, xpeer, ypeer):
         pl.semaphore_signal(barrier, inc=1, device_id=peer, device_id_type=MESH)
@@ -82,27 +76,8 @@
         return (pltpu.make_async_copy(wg_hbm.at[rows, units], wg.at[k], g_sem.at[k]),
                 pltpu.make_async_copy(wu_hbm.at[rows, units], wu.at[k], u_sem.at[k]))
 
-    def w_pieces(k):
-        for p in range(0, KC, KP):
-            rows = pl.ds(k * KC + p, KP)
-            yield pltpu.make_async_copy(wg_hbm.at[rows, units], wg.at[k, pl.ds(p, KP)], g_sem.at[k])
-            yield pltpu.make_async_copy(wu_hbm.at[rows, units], wu.at[k, pl.ds(p, KP)], u_sem.at[k])
-
     def wd_copy(j):
         return pltpu.make_async_copy(wd_hbm.at[units, pl.ds(j * DB, DB)], wd.at[j], w_sem.at[j])
-
-    def wd_pieces(j):
-        for p in range(0, FH, FP):
-            rows = pl.ds(pl.multiple_of(grp * FH + p, FP), FP)
-            yield pltpu.make_async_copy(
-                wd_hbm.at[rows, pl.ds(j * DB, DB)], wd.at[j, pl.ds(p, FP)], w_sem.at[j])
-
-    queue = [c for k in range(NK) for c in w_pieces(k)] + [c for j in range(ND) for c in wd_pieces(j)]
-
-    def more(n):
-        for _ in range(n):
-            if queue:
-                queue.pop(0).start()
 
     def push(src, dst, send, recv, peer):
         return pltpu.make_async_remote_copy(src, dst, send, recv, device_id=peer, device_id_type=MESH)
@@ -154,10 +129,9 @@
             waited.add(("d", j))
             wd_copy(j).wait()
 
-    def gate_up(xref, acc, k, lo, hi, counts, first, h):
+    def gate_up(xref, acc, k, lo, hi, first, h):
         cols = pl.ds(k * KC if isinstance(k, int) else pl.multiple_of(k * KC, KC), KC)
         for n in range(lo, hi, NB):
-            more(counts[(n - lo) // NB])
             nn = pl.ds(n, NB)
             g = jnp.dot(xref[:, cols], wg[k, :, nn], preferred_element_type=F32)
             u = jnp.dot(xref[:, cols], wu[k, :, nn], preferred_element_type=F32)
@@ -170,17 +144,17 @@
             else:
                 h[:, nn] = (jax.nn.silu(g) * u).astype(BF16)
 
-    def own(k, half, counts):
+    def own(k, half):
         wait_w(k)
         if "x" not in waited:
             waited.add("x")
             x_theirs.wait()
         lo = half * (FH // 2)
-        gate_up(xs, acc_s, k, lo, lo + FH // 2, counts, k == 0, h_s if k == NK - 1 else None)
+        gate_up(xs, acc_s, k, lo, lo + FH // 2, k == 0, h_s if k == NK - 1 else None)
 
     slots = [t[1] for t in SCHEDULE if t[0] == "o"]
 
-    def other(slot, counts):
+    def other(slot):
         kind, r = slot[0], int(slot[1])
         if kind == "c":
             wait_w(NR + r)
@@ -193,15 +167,14 @@
             ready = (base + 2 * r, base + 2 * r + 1)
         for i in ready:
             d_x(i).wait_recv()
-        gate_up(xo, acc_o, k, 0, FH, counts, slot == slots[0], h_o if slot == slots[-1] else None)
+        gate_up(xo, acc_o, k, 0, FH, slot == slots[0], h_o if slot == slots[-1] else None)
 
     def block(j):
         return pl.ds(OFFS[j], WIDTHS[j])
 
-    def term(h, acc, tb, j, counts):
+    def term(h, acc, tb, j):
         o, w = OFFS[j], WIDTHS[j]
         wait_wd(o // DB)
-        more(counts[0])
         acc[o // FH, :, pl.ds(o % FH, w)] = jnp.dot(
             h[...], wd[o // DB, :, pl.ds(o % DB, w)], preferred_element_type=F32)
         tb[:, block(j)] = acc[o // FH, theirs, pl.ds(o % FH, w)].astype(BF16)
@@ -243,13 +216,20 @@
         y_ref[mine, block(j)] = (ux[:, block(j)].astype(F32) + xr[:, block(j)].astype(F32)).astype(BF16)
         gather(j).start()
 
-    more(PREFILL)
+    fence()
+    for k in range(NK):
+        for c in w_copies(k):
+            c.start()
+        if k == 0:
+            fence()
+            x_theirs.start()
+        fence()
+    for j in range(ND):
+        wd_copy(j).start()
     pl.semaphore_wait(barrier, 3)
     x_mine.wait()
     for i in range(NR + NC):
         y_x(i).start()
-    x_theirs.start()
-    more(START)
 
     for kind, i, *rest in SCHEDULE:
         if kind == "y":
@@ -270,10 +250,8 @@
             send_y(i)
         elif kind == "c":
             send_x(i)
-        elif kind == "f":
+        else:
             finish(i)
-        else:
-            more(i)
 
     for j in range(NT):
         gather(j).wait_recv()
@@ -311,6 +289,7 @@
             pltpu.VMEM((ROWS, FH), BF16),
             pltpu.VMEM((ROWS, FH), BF16),
             half, half, half, half, half, half, half, half,
+            pltpu.SemaphoreType.REGULAR,
             dma((2,)), dma((NK,)), dma((NK,)), dma((ND,)),
             dma((NR + NC,)), dma((NR + NC,)), dma((NR,)), dma((NR,)),
             dma((2 * NR + NC,)), dma((2 * NR + NC,)),

time: 47.1 us -> 43.9 us (0.932)
  Pallas kernels: 44.7 us -> 41.5 us
    pallas_call x1, Pallas kernels: 44.7 us -> 41.5 us  [mlp(): pl.pallas_call(kernel, name='mlp', out_shape=jax.ShapeDtypeStruct((ROWS,...]
where the time goes in v6:
time: 43.9 us; the launch traced here: 43.8 us
  Pallas kernels  41.5 us (95%)
  local copies, waits for them, and re-layouts  2.29 us (5%)
    pallas_call x1, Pallas kernels, mlp(): pl.pallas_call(kernel, name='mlp', out_shape=jax.ShapeDtypeStruct((ROWS,...  41.5 us
    unnamed x1, local copies, waits for them, and re-layouts  2.29 us

profile of v6, /device:TPU:0, one launch (start us, length us, event | category | flops | bytes accessed | tf_op | source)
XLA Modules:
  0.0 43.8 jit_solution(148004661367083385)
XLA Ops:
  0.0 41.5 %mlp.1 = bf16[128,4096]{1,0:T(8,128)(2,1)} custom-call(bf16[128,4096]{1,0:T(8,128)(2,1)} %x_hbm.1, bf16[4096,4096]{1,0:T(8,128)(2,1)} %wg_hbm.1, bf16[4096,4096]{1,0:T(8,128)(2,1)} %wu_hbm.1, bf16[4096,4096]{1,0:T(8,128)(2,1)} %wd_hbm.1), custom_call_target="tpu_custom_call" | custom-call | tf_op jit(solution)/shard_map/mlp/pallas_call | solution.py:275
  41.5 2.3 %copy.6 = bf16[128,4096]{1,0:T(8,128)(2,1)} copy(bf16[128,4096]{1,0:T(8,128)(2,1)} %mlp.1) | data formatting | bytes 2097152

commit v7 on v6

--- a/solution.py
+++ b/solution.py
@@ -27,14 +27,14 @@
 OFFS = tuple(sum(WIDTHS[:j]) for j in range(NT))
 
 SCHEDULE = (
-    ('s',0,0), ('s',0,1), ('y',0), ('s',1,0), ('s',1,1), ('y',1), ('y',2), ('s',2,0), ('s',2,1), ('y',3),
-    ('o','y0'), ('y',4), ('x',0), ('s',3,0), ('o','y1'), ('y',5), ('x',1), ('s',3,1), ('y',6), ('x',2),
-    ('s',4,0), ('s',4,1), ('y',7), ('x',3), ('o','x0'), ('y',8), ('x',4), ('o','y2'), ('y',9), ('x',5),
-    ('o','x1'), ('o','c0'), ('o','x2'), ('o','c1'), ('t',0), ('t',1), ('t',2), ('s',5,0), ('s',5,1), ('e',0),
-    ('e',1), ('s',6,0), ('t',3), ('e',2), ('s',6,1), ('s',7,0), ('s',7,1), ('t',4), ('e',3), ('S',0), ('S',1),
-    ('S',2), ('t',5), ('e',4), ('S',3), ('c',0), ('c',1), ('S',4), ('S',5), ('c',2), ('t',6), ('e',5), ('S',6),
-    ('t',7), ('S',7), ('c',3), ('t',8), ('e',6), ('f',0), ('S',8), ('t',9), ('e',7), ('S',9), ('f',1), ('c',4),
-    ('e',8), ('e',9), ('f',2), ('c',5), ('f',3), ('c',6), ('f',4), ('c',7), ('c',8), ('f',5), ('c',9), ('f',6),
+    ('s',0,0), ('s',0,1), ('s',1,0), ('y',0), ('s',1,1), ('y',1), ('s',2,0), ('y',2), ('s',2,1), ('y',3),
+    ('s',3,0), ('o','y0'), ('y',4), ('x',0), ('s',3,1), ('y',5), ('x',1), ('o','y1'), ('y',6), ('x',2),
+    ('s',4,0), ('y',7), ('s',4,1), ('x',3), ('s',5,0), ('y',8), ('o','y2'), ('y',9), ('x',4), ('o','x0'),
+    ('x',5), ('o','x1'), ('o','c0'), ('o','c1'), ('o','x2'), ('t',0), ('t',1), ('t',2), ('s',5,1), ('s',6,0),
+    ('s',6,1), ('e',0), ('e',1), ('s',7,0), ('t',3), ('e',2), ('s',7,1), ('S',0), ('S',1), ('t',4), ('S',2),
+    ('e',3), ('S',3), ('t',5), ('c',0), ('S',4), ('c',1), ('S',5), ('e',4), ('t',6), ('S',6), ('c',2), ('t',7),
+    ('e',5), ('S',7), ('t',8), ('S',8), ('e',6), ('c',3), ('f',0), ('t',9), ('S',9), ('f',1), ('e',7), ('e',8),
+    ('c',4), ('e',9), ('c',5), ('f',2), ('c',6), ('f',3), ('c',7), ('f',4), ('c',8), ('f',5), ('c',9), ('f',6),
     ('f',7), ('f',8), ('f',9),
 )
 
@@ -275,7 +275,7 @@
     return pl.pallas_call(
         kernel,
         name="mlp",
-        out_shape=jax.ShapeDtypeStruct((ROWS, D), BF16),
+        out_shape=pltpu.VMEM((ROWS, D), BF16),
         in_specs=[pl.BlockSpec(memory_space=pl.ANY)] * 4,
         out_specs=pl.BlockSpec(memory_space=pltpu.VMEM),
         scratch_shapes=[
@@ -297,7 +297,7 @@
             dma((NT,)), dma((NT,)), dma((NT,)), dma((NT,)),
         ],
         compiler_params=pltpu.CompilerParams(
-            collective_id=0, has_side_effects=True, vmem_limit_bytes=67043328),
+            collective_id=0, has_side_effects=True, vmem_limit_bytes=65011712),
     )(x, w_gate, w_up, w_down)
 
 

time: 43.9 us -> 41.6 us (0.948)
  local copies, waits for them, and re-layouts: 2.29 us -> 0.97 us
  Pallas kernels: 41.5 us -> 40.6 us
    unnamed x1, local copies, waits for them, and re-layouts: 2.29 us -> 0.97 us
    pallas_call x1, Pallas kernels: 41.5 us -> 40.6 us  [mlp(): pl.pallas_call(kernel, name='mlp', out_shape=pltpu.VMEM((ROWS, D), BF16),...]
where the time goes in v7:
time: 41.6 us; the launch traced here: 41.5 us
  Pallas kernels  40.6 us (98%)
  local copies, waits for them, and re-layouts  0.97 us (2%)
    pallas_call x1, Pallas kernels, mlp(): pl.pallas_call(kernel, name='mlp', out_shape=pltpu.VMEM((ROWS, D), BF16),...  40.6 us
    unnamed x1, local copies, waits for them, and re-layouts  0.97 us

profile of v7, /device:TPU:0, one launch (start us, length us, event | category | flops | bytes accessed | tf_op | source)
XLA Modules:
  0.0 41.5 jit_solution(6938069016466846752)
XLA Ops:
  0.0 40.6 %mlp.1 = bf16[128,4096]{1,0:T(8,128)(2,1)S(1)} custom-call(bf16[128,4096]{1,0:T(8,128)(2,1)} %x_hbm.1, bf16[4096,4096]{1,0:T(8,128)(2,1)} %wg_hbm.1, bf16[4096,4096]{1,0:T(8,128)(2,1)} %wu_hbm.1, bf16[4096,4096]{1,0:T(8,128)(2,1)} %wd_hbm.1), custom_call_target="tpu_custom_call" | custom-call | tf_op jit(solution)/shard_map/mlp/pallas_call | solution.py:275
  40.6 1.0 %copy.6 = bf16[128,4096]{1,0:T(8,128)(2,1)} copy(bf16[128,4096]{1,0:T(8,128)(2,1)S(1)} %mlp.1) | data formatting | bytes 2097152

commit v8 on v7

--- a/solution.py
+++ b/solution.py
@@ -22,20 +22,20 @@
 DB = 512
 ND = D // DB
 XP = 16
-WIDTHS = (256, 256, 512, 512, 512, 512, 512, 512, 256, 256)
+WIDTHS = (256, 256, 512, 512, 512, 512, 512, 512, 256, 128, 128)
 NT = len(WIDTHS)
 OFFS = tuple(sum(WIDTHS[:j]) for j in range(NT))
 
 SCHEDULE = (
-    ('s',0,0), ('s',0,1), ('s',1,0), ('y',0), ('s',1,1), ('y',1), ('s',2,0), ('y',2), ('s',2,1), ('y',3),
-    ('s',3,0), ('o','y0'), ('y',4), ('x',0), ('s',3,1), ('y',5), ('x',1), ('o','y1'), ('y',6), ('x',2),
-    ('s',4,0), ('y',7), ('s',4,1), ('x',3), ('s',5,0), ('y',8), ('o','y2'), ('y',9), ('x',4), ('o','x0'),
-    ('x',5), ('o','x1'), ('o','c0'), ('o','c1'), ('o','x2'), ('t',0), ('t',1), ('t',2), ('s',5,1), ('s',6,0),
-    ('s',6,1), ('e',0), ('e',1), ('s',7,0), ('t',3), ('e',2), ('s',7,1), ('S',0), ('S',1), ('t',4), ('S',2),
-    ('e',3), ('S',3), ('t',5), ('c',0), ('S',4), ('c',1), ('S',5), ('e',4), ('t',6), ('S',6), ('c',2), ('t',7),
-    ('e',5), ('S',7), ('t',8), ('S',8), ('e',6), ('c',3), ('f',0), ('t',9), ('S',9), ('f',1), ('e',7), ('e',8),
-    ('c',4), ('e',9), ('c',5), ('f',2), ('c',6), ('f',3), ('c',7), ('f',4), ('c',8), ('f',5), ('c',9), ('f',6),
-    ('f',7), ('f',8), ('f',9),
+    ('s',0,0), ('s',0,1), ('s',1,0), ('y',0), ('s',1,1), ('y',1), ('s',2,0), ('s',2,1), ('y',2), ('s',3,0),
+    ('y',3), ('o','y0'), ('y',4), ('s',3,1), ('y',5), ('x',0), ('s',4,0), ('x',1), ('o','y1'), ('y',6),
+    ('s',4,1), ('y',7), ('x',2), ('o','y2'), ('x',3), ('y',8), ('o','x0'), ('y',9), ('x',4), ('o','c0'),
+    ('x',5), ('o','x1'), ('o','c1'), ('o','x2'), ('t',0), ('t',1), ('t',2), ('s',5,0), ('s',5,1), ('e',0),
+    ('s',6,0), ('e',1), ('t',3), ('s',6,1), ('e',2), ('s',7,0), ('s',7,1), ('t',4), ('S',0), ('e',3), ('S',1),
+    ('S',2), ('t',5), ('e',4), ('c',0), ('S',3), ('c',1), ('S',4), ('t',6), ('e',5), ('c',2), ('t',7), ('t',8),
+    ('c',3), ('e',6), ('S',5), ('S',6), ('t',9), ('f',0), ('f',1), ('c',4), ('e',7), ('c',5), ('e',8), ('S',7),
+    ('t',10), ('S',8), ('c',6), ('e',9), ('S',9), ('f',2), ('e',10), ('f',3), ('c',7), ('f',4), ('c',8),
+    ('S',10), ('c',9), ('c',10), ('f',5), ('f',6), ('f',7), ('f',8), ('f',9), ('f',10),
 )
 
 

time: 41.6 us -> 40.2 us (0.966)
  Pallas kernels: 40.6 us -> 39.2 us
    pallas_call x1, Pallas kernels: 40.6 us -> 39.2 us  [mlp(): pl.pallas_call(kernel, name='mlp', out_shape=pltpu.VMEM((ROWS, D), BF16),...]
where the time goes in v8:
time: 40.2 us
  Pallas kernels  39.2 us (98%)
  local copies, waits for them, and re-layouts  0.97 us (2%)
    pallas_call x1, Pallas kernels, mlp(): pl.pallas_call(kernel, name='mlp', out_shape=pltpu.VMEM((ROWS, D), BF16),...  39.2 us
    unnamed x1, local copies, waits for them, and re-layouts  0.97 us

profile of v8, /device:TPU:0, one launch (start us, length us, event | category | flops | bytes accessed | tf_op | source)
XLA Modules:
  0.0 40.2 jit_solution(5527030318864198286)
XLA Ops:
  0.0 39.2 %mlp.1 = bf16[128,4096]{1,0:T(8,128)(2,1)S(1)} custom-call(bf16[128,4096]{1,0:T(8,128)(2,1)} %x_hbm.1, bf16[4096,4096]{1,0:T(8,128)(2,1)} %wg_hbm.1, bf16[4096,4096]{1,0:T(8,128)(2,1)} %wu_hbm.1, bf16[4096,4096]{1,0:T(8,128)(2,1)} %wd_hbm.1), custom_call_target="tpu_custom_call" | custom-call | tf_op jit(solution)/shard_map/mlp/pallas_call | solution.py:275
  39.2 1.0 %copy.6 = bf16[128,4096]{1,0:T(8,128)(2,1)} copy(bf16[128,4096]{1,0:T(8,128)(2,1)S(1)} %mlp.1) | data formatting | bytes 2097152

commit v9 on v8

--- a/solution.py
+++ b/solution.py
@@ -22,20 +22,23 @@
 DB = 512
 ND = D // DB
 XP = 16
-WIDTHS = (256, 256, 512, 512, 512, 512, 512, 512, 256, 128, 128)
+WIDTHS = (256, 256, 256, 256, 256, 256, 256, 256, 256, 256, 256, 256, 256, 256, 128, 128, 128, 128)
 NT = len(WIDTHS)
 OFFS = tuple(sum(WIDTHS[:j]) for j in range(NT))
 
 SCHEDULE = (
-    ('s',0,0), ('s',0,1), ('s',1,0), ('y',0), ('s',1,1), ('y',1), ('s',2,0), ('s',2,1), ('y',2), ('s',3,0),
-    ('y',3), ('o','y0'), ('y',4), ('s',3,1), ('y',5), ('x',0), ('s',4,0), ('x',1), ('o','y1'), ('y',6),
-    ('s',4,1), ('y',7), ('x',2), ('o','y2'), ('x',3), ('y',8), ('o','x0'), ('y',9), ('x',4), ('o','c0'),
-    ('x',5), ('o','x1'), ('o','c1'), ('o','x2'), ('t',0), ('t',1), ('t',2), ('s',5,0), ('s',5,1), ('e',0),
-    ('s',6,0), ('e',1), ('t',3), ('s',6,1), ('e',2), ('s',7,0), ('s',7,1), ('t',4), ('S',0), ('e',3), ('S',1),
-    ('S',2), ('t',5), ('e',4), ('c',0), ('S',3), ('c',1), ('S',4), ('t',6), ('e',5), ('c',2), ('t',7), ('t',8),
-    ('c',3), ('e',6), ('S',5), ('S',6), ('t',9), ('f',0), ('f',1), ('c',4), ('e',7), ('c',5), ('e',8), ('S',7),
-    ('t',10), ('S',8), ('c',6), ('e',9), ('S',9), ('f',2), ('e',10), ('f',3), ('c',7), ('f',4), ('c',8),
-    ('S',10), ('c',9), ('c',10), ('f',5), ('f',6), ('f',7), ('f',8), ('f',9), ('f',10),
+    ('s',0,2), ('y',0), ('s',1,2), ('y',1), ('s',2,2), ('y',2), ('y',3), ('s',3,2), ('y',4), ('o','y0'),
+    ('y',5), ('x',0), ('o','y1'), ('x',1), ('y',6), ('s',4,2), ('y',7), ('x',2), ('o','y2'), ('x',3), ('y',8),
+    ('o','x0'), ('y',9), ('x',4), ('o','c0'), ('x',5), ('o','x1'), ('o','c1'), ('o','x2'), ('t',0), ('t',1),
+    ('t',2), ('t',3), ('s',5,2), ('e',0), ('t',4), ('e',1), ('s',6,2), ('e',2), ('e',3), ('s',7,2), ('t',5),
+    ('S',0), ('S',1), ('e',4), ('t',6), ('t',7), ('t',8), ('S',2), ('c',0), ('e',5), ('t',9), ('S',3), ('c',1),
+    ('e',6), ('e',7), ('t',10), ('S',4), ('c',2), ('e',8), ('S',5), ('t',11), ('c',3), ('S',6), ('t',12),
+    ('e',9), ('c',4), ('e',10), ('S',7), ('t',13), ('c',5), ('e',11), ('t',14), ('f',0), ('S',8), ('c',6),
+    ('t',15), ('S',9), ('e',12), ('c',7), ('S',10), ('S',11), ('e',13), ('e',14), ('c',8), ('f',1), ('t',16),
+    ('f',2), ('S',12), ('e',15), ('c',9), ('t',17), ('S',13), ('S',14), ('c',10), ('f',3), ('e',16), ('S',15),
+    ('f',4), ('c',11), ('e',17), ('S',16), ('S',17), ('c',12), ('c',13), ('c',14), ('c',15), ('c',16), ('f',5),
+    ('f',6), ('f',7), ('c',17), ('f',8), ('f',9), ('f',10), ('f',11), ('f',12), ('f',13), ('f',14), ('f',15),
+    ('f',16), ('f',17),
 )
 
 
@@ -149,8 +152,8 @@
         if "x" not in waited:
             waited.add("x")
             x_theirs.wait()
-        lo = half * (FH // 2)
-        gate_up(xs, acc_s, k, lo, lo + FH // 2, k == 0, h_s if k == NK - 1 else None)
+        lo, hi = (0, FH) if half == 2 else (half * (FH // 2), (half + 1) * (FH // 2))
+        gate_up(xs, acc_s, k, lo, hi, k == 0, h_s if k == NK - 1 else None)
 
     slots = [t[1] for t in SCHEDULE if t[0] == "o"]
 

time: 40.2 us -> 43.8 us (1.090)
  Pallas kernels: 39.2 us -> 42.7 us
    pallas_call x1, Pallas kernels: 39.2 us -> 42.7 us  [mlp(): pl.pallas_call(kernel, name='mlp', out_shape=pltpu.VMEM((ROWS, D), BF16),...]
where the time goes in v9:
time: 43.8 us; the launch traced here: 43.7 us
  Pallas kernels  42.7 us (97%)
  local copies, waits for them, and re-layouts  0.97 us (2%)
    pallas_call x1, Pallas kernels, mlp(): pl.pallas_call(kernel, name='mlp', out_shape=pltpu.VMEM((ROWS, D), BF16),...  42.7 us
    unnamed x1, local copies, waits for them, and re-layouts  0.97 us

profile of v9, /device:TPU:0, one launch (start us, length us, event | category | flops | bytes accessed | tf_op | source)
XLA Modules:
  0.0 43.7 jit_solution(1398473156357747219)
XLA Ops:
  0.0 42.7 %mlp.1 = bf16[128,4096]{1,0:T(8,128)(2,1)S(1)} custom-call(bf16[128,4096]{1,0:T(8,128)(2,1)} %x_hbm.1, bf16[4096,4096]{1,0:T(8,128)(2,1)} %wg_hbm.1, bf16[4096,4096]{1,0:T(8,128)(2,1)} %wu_hbm.1, bf16[4096,4096]{1,0:T(8,128)(2,1)} %wd_hbm.1), custom_call_target="tpu_custom_call" | custom-call | tf_op jit(solution)/shard_map/mlp/pallas_call | solution.py:278
  42.7 1.0 %copy.6 = bf16[128,4096]{1,0:T(8,128)(2,1)} copy(bf16[128,4096]{1,0:T(8,128)(2,1)S(1)} %mlp.1) | data formatting | bytes 2097152

commit v10 on v8

--- a/solution.py
+++ b/solution.py
@@ -20,8 +20,9 @@
 NC = 4
 NB = 256
 DB = 512
+TU = 128
 ND = D // DB
-XP = 16
+NX = D // XC
 WIDTHS = (256, 256, 512, 512, 512, 512, 512, 512, 256, 128, 128)
 NT = len(WIDTHS)
 OFFS = tuple(sum(WIDTHS[:j]) for j in range(NT))
@@ -65,11 +66,10 @@
     for peer in (partner, xpeer, ypeer):
         pl.semaphore_signal(barrier, inc=1, device_id=peer, device_id_type=MESH)
 
-    for p in range(0, HALF, XP):
-        rows = pl.ds(pl.multiple_of(core * HALF + p, XP), XP)
-        pltpu.make_async_copy(x_hbm.at[rows], xs.at[rows], x_sem.at[0]).start()
-    x_mine = pltpu.make_async_copy(x_hbm.at[mine], xs.at[mine], x_sem.at[0])
-    x_theirs = pltpu.make_async_copy(x_hbm.at[theirs], xs.at[theirs], x_sem.at[1])
+    def x_read(u, rows, q):
+        cols = pl.ds(u * XC if isinstance(u, int) else pl.multiple_of(u * XC, XC), XC)
+        return pltpu.make_async_copy(x_hbm.at[rows, cols], xs.at[u, rows], x_sem.at[q, u])
+
 
     def w_copies(k):
         rows = pl.ds(k * KC, KC)
@@ -85,25 +85,23 @@
     def relay_k(i, c):
         return 2 * (i // 2) + c
 
-    def relay_cols(i, c):
-        return pl.ds(pl.multiple_of(relay_k(i, c) * KC + (i % 2) * XC, XC), XC)
-
-    def y_cols(i):
-        if i < NR:
-            return relay_cols(i, chip)
-        return pl.ds(2 * NR * XC + (i - NR) * XC, XC)
+    def relay_u(i, c):
+        return 2 * relay_k(i, c) + i % 2
+
+    def y_unit(i):
+        return relay_u(i, chip) if i < NR else NR + i
 
     def y_x(i):
-        c = y_cols(i)
-        return push(xs.at[mine, c], xo.at[mine, c], yx_send.at[i], yx_recv.at[i], ypeer)
+        u = y_unit(i)
+        return push(xs.at[u, mine], xo.at[u, mine], yx_send.at[i], yx_recv.at[i], ypeer)
 
     def x_x(i, c):
-        c = relay_cols(i, c)
-        return push(xo.at[mine, c], xo.at[mine, c], xx_send.at[i], xx_recv.at[i], xpeer)
+        u = relay_u(i, c)
+        return push(xo.at[u, mine], xo.at[u, mine], xx_send.at[i], xx_recv.at[i], xpeer)
 
     def d_x(i):
-        c = y_cols(i) if i < NR + NC else relay_cols(i - NR - NC, 1 - chip)
-        return push(xo.at[mine, c], xo.at[mine, c], dx_send.at[i], dx_recv.at[i], partner)
+        u = y_unit(i) if i < NR + NC else relay_u(i - NR - NC, 1 - chip)
+        return push(xo.at[u, mine], xo.at[u, mine], dx_send.at[i], dx_recv.at[i], partner)
 
     def on_y(i):
         y_x(i).wait_recv()
@@ -130,11 +128,11 @@
             wd_copy(j).wait()
 
     def gate_up(xref, acc, k, lo, hi, first, h):
-        cols = pl.ds(k * KC if isinstance(k, int) else pl.multiple_of(k * KC, KC), KC)
+        lhs = jnp.concatenate([xref[2 * k], xref[2 * k + 1]], axis=1)
         for n in range(lo, hi, NB):
             nn = pl.ds(n, NB)
-            g = jnp.dot(xref[:, cols], wg[k, :, nn], preferred_element_type=F32)
-            u = jnp.dot(xref[:, cols], wu[k, :, nn], preferred_element_type=F32)
+            g = jnp.dot(lhs, wg[k, :, nn], preferred_element_type=F32)
+            u = jnp.dot(lhs, wu[k, :, nn], preferred_element_type=F32)
             if not first:
                 g = acc[0, :, nn] + g
                 u = acc[1, :, nn] + u
@@ -148,9 +146,12 @@
         wait_w(k)
         if "x" not in waited:
             waited.add("x")
-            x_theirs.wait()
-        lo = half * (FH // 2)
-        gate_up(xs, acc_s, k, lo, lo + FH // 2, k == 0, h_s if k == NK - 1 else None)
+            for i in range(NR):
+                x_read(relay_u(i, 1 - chip), mine, 0).wait()
+            for u in range(NX):
+                x_read(u, theirs, 1).wait()
+        lo, hi = (0, FH) if half == 2 else (half * (FH // 2), (half + 1) * (FH // 2))
+        gate_up(xs, acc_s, k, lo, hi, k == 0, h_s if k == NK - 1 else None)
 
     slots = [t[1] for t in SCHEDULE if t[0] == "o"]
 
@@ -172,28 +173,35 @@
     def block(j):
         return pl.ds(OFFS[j], WIDTHS[j])
 
+    def units_of(j):
+        return pl.ds(OFFS[j] // TU, WIDTHS[j] // TU)
+
+    def lanes(j):
+        for o in range(OFFS[j], OFFS[j] + WIDTHS[j], TU):
+            yield o // TU, o // FH, pl.ds(o % FH, TU)
+
     def term(h, acc, tb, j):
         o, w = OFFS[j], WIDTHS[j]
         wait_wd(o // DB)
         acc[o // FH, :, pl.ds(o % FH, w)] = jnp.dot(
             h[...], wd[o // DB, :, pl.ds(o % DB, w)], preferred_element_type=F32)
-        tb[:, block(j)] = acc[o // FH, theirs, pl.ds(o % FH, w)].astype(BF16)
-
-    def part(acc, j):
-        o, w = OFFS[j], WIDTHS[j]
-        return acc[o // FH, mine, pl.ds(o % FH, w)]
+        for u, q, cc in lanes(j):
+            tb[u] = acc[q, theirs, cc].astype(BF16)
+
+    def hop(src, dst, send, recv, j, peer):
+        return push(src.at[units_of(j)], dst.at[units_of(j)], send.at[j], recv.at[j], peer)
 
     def core_o(j):
-        return push(tb_o.at[:, block(j)], rb_o.at[:, block(j)], do_send.at[j], do_recv.at[j], partner)
+        return hop(tb_o, rb_o, do_send, do_recv, j, partner)
 
     def core_s(j):
-        return push(tb_s.at[:, block(j)], rb_s.at[:, block(j)], ds_send.at[j], ds_recv.at[j], partner)
+        return hop(tb_s, rb_s, ds_send, ds_recv, j, partner)
 
     def over_y(j):
-        return push(uy.at[:, block(j)], yr.at[:, block(j)], uy_send.at[j], uy_recv.at[j], ypeer)
+        return hop(uy, yr, uy_send, uy_recv, j, ypeer)
 
     def over_x(j):
-        return push(ux.at[:, block(j)], xr.at[:, block(j)], ux_send.at[j], ux_recv.at[j], xpeer)
+        return hop(ux, xr, ux_send, ux_recv, j, xpeer)
 
     def gather(j):
         rows = y_ref.at[mine, block(j)]
@@ -201,34 +209,42 @@
 
     def send_y(j):
         core_o(j).wait_recv()
-        uy[:, block(j)] = (part(acc_o, j) + rb_o[:, block(j)].astype(F32)).astype(BF16)
+        for u, q, cc in lanes(j):
+            uy[u] = (acc_o[q, mine, cc] + rb_o[u].astype(F32)).astype(BF16)
         over_y(j).start()
 
     def send_x(j):
         core_s(j).wait_recv()
         over_y(j).wait_recv()
-        ux[:, block(j)] = (part(acc_s, j) + rb_s[:, block(j)].astype(F32)
-                           + yr[:, block(j)].astype(F32)).astype(BF16)
+        for u, q, cc in lanes(j):
+            ux[u] = (acc_s[q, mine, cc] + rb_s[u].astype(F32) + yr[u].astype(F32)).astype(BF16)
         over_x(j).start()
 
     def finish(j):
         over_x(j).wait_recv()
-        y_ref[mine, block(j)] = (ux[:, block(j)].astype(F32) + xr[:, block(j)].astype(F32)).astype(BF16)
+        for u, q, cc in lanes(j):
+            y_ref[mine, pl.ds(u * TU, TU)] = (ux[u].astype(F32) + xr[u].astype(F32)).astype(BF16)
         gather(j).start()
 
+    sent = tuple(y_unit(i) for i in range(NR + NC))
+    for u in sent:
+        x_read(u, mine, 0).start()
     fence()
     for k in range(NK):
         for c in w_copies(k):
             c.start()
         if k == 0:
             fence()
-            x_theirs.start()
+            for i in range(NR):
+                x_read(relay_u(i, 1 - chip), mine, 0).start()
+            for u in range(NX):
+                x_read(u, theirs, 1).start()
         fence()
     for j in range(ND):
         wd_copy(j).start()
     pl.semaphore_wait(barrier, 3)
-    x_mine.wait()
-    for i in range(NR + NC):
+    for i, u in enumerate(sent):
+        x_read(u, mine, 0).wait()
         y_x(i).start()
 
     for kind, i, *rest in SCHEDULE:
@@ -271,7 +287,7 @@
 
 def mlp(x, w_gate, w_up, w_down):
     dma = pltpu.SemaphoreType.DMA
-    half = pltpu.VMEM((HALF, D), BF16)
+    half = pltpu.VMEM((D // TU, HALF, TU), BF16)
     return pl.pallas_call(
         kernel,
         name="mlp",
@@ -279,8 +295,8 @@
         in_specs=[pl.BlockSpec(memory_space=pl.ANY)] * 4,
         out_specs=pl.BlockSpec(memory_space=pltpu.VMEM),
         scratch_shapes=[
-            pltpu.VMEM((ROWS, D), BF16),
-            pltpu.VMEM((ROWS, D), BF16),
+            pltpu.VMEM((NX, ROWS, XC), BF16),
+            pltpu.VMEM((NX, ROWS, XC), BF16),
             pltpu.VMEM((NK, KC, FH), BF16),
             pltpu.VMEM((NK, KC, FH), BF16),
             pltpu.VMEM((ND, FH, DB), BF16),
@@ -290,7 +306,7 @@
             pltpu.VMEM((ROWS, FH), BF16),
             half, half, half, half, half, half, half, half,
             pltpu.SemaphoreType.REGULAR,
-            dma((2,)), dma((NK,)), dma((NK,)), dma((ND,)),
+            dma((2, NX)), dma((NK,)), dma((NK,)), dma((ND,)),
             dma((NR + NC,)), dma((NR + NC,)), dma((NR,)), dma((NR,)),
             dma((2 * NR + NC,)), dma((2 * NR + NC,)),
             dma((NT,)), dma((NT,)), dma((NT,)), dma((NT,)), dma((NT,)), dma((NT,)),

time: 40.2 us -> 40.2 us (level)
  no operation moved by 1% of the time
where the time goes in v10:
time: 40.2 us; the launch traced here: 40.1 us
  Pallas kernels  39.1 us (97%)
  local copies, waits for them, and re-layouts  0.97 us (2%)
    pallas_call x1, Pallas kernels, mlp(): pl.pallas_call(kernel, name='mlp', out_shape=pltpu.VMEM((ROWS, D), BF16),...  39.1 us
    unnamed x1, local copies, waits for them, and re-layouts  0.97 us

profile of v10, /device:TPU:0, one launch (start us, length us, event | category | flops | bytes accessed | tf_op | source)
XLA Modules:
  0.0 40.1 jit_solution(1751293942814450058)
XLA Ops:
  0.0 39.1 %mlp.1 = bf16[128,4096]{1,0:T(8,128)(2,1)S(1)} custom-call(bf16[128,4096]{1,0:T(8,128)(2,1)} %x_hbm.1, bf16[4096,4096]{1,0:T(8,128)(2,1)} %wg_hbm.1, bf16[4096,4096]{1,0:T(8,128)(2,1)} %wu_hbm.1, bf16[4096,4096]{1,0:T(8,128)(2,1)} %wd_hbm.1), custom_call_target="tpu_custom_call" | custom-call | tf_op jit(solution)/shard_map/mlp/pallas_call | solution.py:291
  39.1 1.0 %copy.6 = bf16[128,4096]{1,0:T(8,128)(2,1)} copy(bf16[128,4096]{1,0:T(8,128)(2,1)S(1)} %mlp.1) | data formatting | bytes 2097152

commit v11 on v10

--- a/solution.py
+++ b/solution.py
@@ -23,20 +23,25 @@
 TU = 128
 ND = D // DB
 NX = D // XC
-WIDTHS = (256, 256, 512, 512, 512, 512, 512, 512, 256, 128, 128)
+WIDTHS = (512, 512, 512, 512, 512, 512, 512, 512)
 NT = len(WIDTHS)
 OFFS = tuple(sum(WIDTHS[:j]) for j in range(NT))
+OWN_W = (512, 512, 1024, 1024, 1024)
+NS = len(OWN_W)
+OWN_O = tuple(sum(OWN_W[:j]) for j in range(NS))
+OUT_W = (1024, 1024, 1024, 512, 512)
+NG = len(OUT_W)
+OUT_O = tuple(sum(OUT_W[:j]) for j in range(NG))
 
 SCHEDULE = (
-    ('s',0,0), ('s',0,1), ('s',1,0), ('y',0), ('s',1,1), ('y',1), ('s',2,0), ('s',2,1), ('y',2), ('s',3,0),
-    ('y',3), ('o','y0'), ('y',4), ('s',3,1), ('y',5), ('x',0), ('s',4,0), ('x',1), ('o','y1'), ('y',6),
-    ('s',4,1), ('y',7), ('x',2), ('o','y2'), ('x',3), ('y',8), ('o','x0'), ('y',9), ('x',4), ('o','c0'),
-    ('x',5), ('o','x1'), ('o','c1'), ('o','x2'), ('t',0), ('t',1), ('t',2), ('s',5,0), ('s',5,1), ('e',0),
-    ('s',6,0), ('e',1), ('t',3), ('s',6,1), ('e',2), ('s',7,0), ('s',7,1), ('t',4), ('S',0), ('e',3), ('S',1),
-    ('S',2), ('t',5), ('e',4), ('c',0), ('S',3), ('c',1), ('S',4), ('t',6), ('e',5), ('c',2), ('t',7), ('t',8),
-    ('c',3), ('e',6), ('S',5), ('S',6), ('t',9), ('f',0), ('f',1), ('c',4), ('e',7), ('c',5), ('e',8), ('S',7),
-    ('t',10), ('S',8), ('c',6), ('e',9), ('S',9), ('f',2), ('e',10), ('f',3), ('c',7), ('f',4), ('c',8),
-    ('S',10), ('c',9), ('c',10), ('f',5), ('f',6), ('f',7), ('f',8), ('f',9), ('f',10),
+    ('s',0,0), ('s',0,1), ('y',0), ('s',1,0), ('y',1), ('s',1,1), ('s',2,0), ('y',2), ('s',2,1), ('o','y0'),
+    ('y',3), ('s',3,0), ('x',0), ('s',3,1), ('y',4), ('x',1), ('o','y1'), ('y',5), ('s',4,0), ('o','x0'),
+    ('y',6), ('s',4,1), ('y',7), ('x',2), ('x',3), ('o','y2'), ('y',8), ('x',4), ('x',5), ('o','c0'), ('y',9),
+    ('o','x1'), ('o','x2'), ('o','c1'), ('t',0), ('t',1), ('s',5,0), ('s',5,1), ('e',0), ('s',6,0), ('s',6,1),
+    ('e',1), ('t',2), ('s',7,0), ('s',7,1), ('S',0), ('t',3), ('e',2), ('S',1), ('c',0), ('t',4), ('e',3),
+    ('S',2), ('c',1), ('t',5), ('e',4), ('S',3), ('c',2), ('t',6), ('e',5), ('c',3), ('t',7), ('e',6), ('c',4),
+    ('e',7), ('S',4), ('f',0), ('f',1), ('c',5), ('c',6), ('f',2), ('c',7), ('f',3), ('g',0), ('f',4), ('g',1),
+    ('f',5), ('g',2), ('f',6), ('g',3), ('f',7), ('g',4),
 )
 
 
@@ -99,19 +104,25 @@
         u = relay_u(i, c)
         return push(xo.at[u, mine], xo.at[u, mine], xx_send.at[i], xx_recv.at[i], xpeer)
 
-    def d_x(i):
-        u = y_unit(i) if i < NR + NC else relay_u(i - NR - NC, 1 - chip)
-        return push(xo.at[u, mine], xo.at[u, mine], dx_send.at[i], dx_recv.at[i], partner)
+    def d_x(m):
+        if 2 * m < NR + NC:
+            u = y_unit(2 * m)
+        else:
+            u = relay_u(2 * m - NR - NC, 1 - chip)
+        both = xo.at[pl.ds(u, 2), mine]
+        return push(both, both, dx_send.at[m], dx_recv.at[m], partner)
 
     def on_y(i):
         y_x(i).wait_recv()
         if i < NR:
             x_x(i, chip).start()
-        d_x(i).start()
+        if i % 2:
+            d_x(i // 2).start()
 
     def on_x(i):
         x_x(i, 1 - chip).wait_recv()
-        d_x(NR + NC + i).start()
+        if i % 2:
+            d_x((NR + NC + i) // 2).start()
 
     waited = set()
 
@@ -160,71 +171,68 @@
         if kind == "c":
             wait_w(NR + r)
             k = NR + r
-            ready = (NR + 2 * r, NR + 2 * r + 1)
+            ready = NR // 2 + r
         else:
             wait_w(2 * r, 2 * r + 1)
             k = relay_k(2 * r, chip if kind == "y" else 1 - chip)
-            base = 0 if kind == "y" else NR + NC
-            ready = (base + 2 * r, base + 2 * r + 1)
-        for i in ready:
-            d_x(i).wait_recv()
+            ready = r if kind == "y" else (NR + NC) // 2 + r
+        d_x(ready).wait_recv()
         gate_up(xo, acc_o, k, 0, FH, slot == slots[0], h_o if slot == slots[-1] else None)
 
-    def block(j):
-        return pl.ds(OFFS[j], WIDTHS[j])
-
-    def units_of(j):
-        return pl.ds(OFFS[j] // TU, WIDTHS[j] // TU)
-
-    def lanes(j):
-        for o in range(OFFS[j], OFFS[j] + WIDTHS[j], TU):
-            yield o // TU, o // FH, pl.ds(o % FH, TU)
-
-    def term(h, acc, tb, j):
-        o, w = OFFS[j], WIDTHS[j]
-        wait_wd(o // DB)
-        acc[o // FH, :, pl.ds(o % FH, w)] = jnp.dot(
-            h[...], wd[o // DB, :, pl.ds(o % DB, w)], preferred_element_type=F32)
-        for u, q, cc in lanes(j):
+    def lanes(o, w):
+        for p in range(o, o + w, TU):
+            yield p // TU, p // FH, pl.ds(p % FH, TU)
+
+    def term(h, acc, tb, o, w):
+        for p in range(o, o + w, DB):
+            wait_wd(p // DB)
+        for p in range(o, o + w, min(w, DB)):
+            n = min(w, DB)
+            acc[p // FH, :, pl.ds(p % FH, n)] = jnp.dot(
+                h[...], wd[p // DB, :, pl.ds(p % DB, n)], preferred_element_type=F32)
+        for u, q, cc in lanes(o, w):
             tb[u] = acc[q, theirs, cc].astype(BF16)
 
-    def hop(src, dst, send, recv, j, peer):
-        return push(src.at[units_of(j)], dst.at[units_of(j)], send.at[j], recv.at[j], peer)
+    def hop(src, dst, send, recv, j, o, w, peer):
+        units = pl.ds(o // TU, w // TU)
+        return push(src.at[units], dst.at[units], send.at[j], recv.at[j], peer)
 
     def core_o(j):
-        return hop(tb_o, rb_o, do_send, do_recv, j, partner)
+        return hop(tb_o, rb_o, do_send, do_recv, j, OFFS[j], WIDTHS[j], partner)
 
     def core_s(j):
-        return hop(tb_s, rb_s, ds_send, ds_recv, j, partner)
+        return hop(tb_s, rb_s, ds_send, ds_recv, j, OWN_O[j], OWN_W[j], partner)
 
     def over_y(j):
-        return hop(uy, yr, uy_send, uy_recv, j, ypeer)
+        return hop(uy, yr, uy_send, uy_recv, j, OFFS[j], WIDTHS[j], ypeer)
 
     def over_x(j):
-        return hop(ux, xr, ux_send, ux_recv, j, xpeer)
+        return hop(ux, xr, ux_send, ux_recv, j, OFFS[j], WIDTHS[j], xpeer)
 
     def gather(j):
-        rows = y_ref.at[mine, block(j)]
+        rows = y_ref.at[mine, pl.ds(OUT_O[j], OUT_W[j])]
         return push(rows, rows, gy_send.at[j], gy_recv.at[j], partner)
 
     def send_y(j):
         core_o(j).wait_recv()
-        for u, q, cc in lanes(j):
+        for u, q, cc in lanes(OFFS[j], WIDTHS[j]):
             uy[u] = (acc_o[q, mine, cc] + rb_o[u].astype(F32)).astype(BF16)
         over_y(j).start()
 
     def send_x(j):
-        core_s(j).wait_recv()
+        for m in range(NS):
+            if OWN_O[m] < OFFS[j] + WIDTHS[j] and OWN_O[m] + OWN_W[m] > OFFS[j] and ("s", m) not in waited:
+                waited.add(("s", m))
+                core_s(m).wait_recv()
         over_y(j).wait_recv()
-        for u, q, cc in lanes(j):
+        for u, q, cc in lanes(OFFS[j], WIDTHS[j]):
             ux[u] = (acc_s[q, mine, cc] + rb_s[u].astype(F32) + yr[u].astype(F32)).astype(BF16)
         over_x(j).start()
 
     def finish(j):
         over_x(j).wait_recv()
-        for u, q, cc in lanes(j):
+        for u, q, cc in lanes(OFFS[j], WIDTHS[j]):
             y_ref[mine, pl.ds(u * TU, TU)] = (ux[u].astype(F32) + xr[u].astype(F32)).astype(BF16)
-        gather(j).start()
 
     sent = tuple(y_unit(i) for i in range(NR + NC))
     for u in sent:
@@ -257,31 +265,35 @@
         elif kind == "o":
             other(i, *rest)
         elif kind == "t":
-            term(h_o, acc_o, tb_o, i, *rest)
+            term(h_o, acc_o, tb_o, OFFS[i], WIDTHS[i])
             core_o(i).start()
         elif kind == "S":
-            term(h_s, acc_s, tb_s, i, *rest)
+            term(h_s, acc_s, tb_s, OWN_O[i], OWN_W[i])
             core_s(i).start()
         elif kind == "e":
             send_y(i)
         elif kind == "c":
             send_x(i)
+        elif kind == "f":
+            finish(i)
         else:
-            finish(i)
-
-    for j in range(NT):
+            gather(i).start()
+
+    for j in range(NG):
         gather(j).wait_recv()
     for i in range(NR + NC):
         y_x(i).wait_send()
-        d_x(i).wait_send()
     for i in range(NR):
         x_x(i, chip).wait_send()
-        d_x(NR + NC + i).wait_send()
+    for m in range(NX // 2):
+        d_x(m).wait_send()
     for j in range(NT):
         core_o(j).wait_send()
-        core_s(j).wait_send()
         over_y(j).wait_send()
         over_x(j).wait_send()
+    for j in range(NS):
+        core_s(j).wait_send()
+    for j in range(NG):
         gather(j).wait_send()
 
 
@@ -308,9 +320,9 @@
             pltpu.SemaphoreType.REGULAR,
             dma((2, NX)), dma((NK,)), dma((NK,)), dma((ND,)),
             dma((NR + NC,)), dma((NR + NC,)), dma((NR,)), dma((NR,)),
-            dma((2 * NR + NC,)), dma((2 * NR + NC,)),
-            dma((NT,)), dma((NT,)), dma((NT,)), dma((NT,)), dma((NT,)), dma((NT,)),
-            dma((NT,)), dma((NT,)), dma((NT,)), dma((NT,)),
+            dma((NX // 2,)), dma((NX // 2,)),
+            dma((NT,)), dma((NT,)), dma((NT,)), dma((NT,)), dma((NS,)), dma((NS,)),
+            dma((NT,)), dma((NT,)), dma((NG,)), dma((NG,)),
         ],
         compiler_params=pltpu.CompilerParams(
             collective_id=0, has_side_effects=True, vmem_limit_bytes=65011712),

time: 40.2 us -> 39.4 us (0.980)
  Pallas kernels: 39.1 us -> 38.3 us
    pallas_call x1, Pallas kernels: 39.1 us -> 38.3 us  [mlp(): pl.pallas_call(kernel, name='mlp', out_shape=pltpu.VMEM((ROWS, D), BF16),...]
where the time goes in v11:
time: 39.4 us; the launch traced here: 39.3 us
  Pallas kernels  38.3 us (97%)
  local copies, waits for them, and re-layouts  0.97 us (2%)
    pallas_call x1, Pallas kernels, mlp(): pl.pallas_call(kernel, name='mlp', out_shape=pltpu.VMEM((ROWS, D), BF16),...  38.3 us
    unnamed x1, local copies, waits for them, and re-layouts  0.97 us

profile of v11, /device:TPU:0, one launch (start us, length us, event | category | flops | bytes accessed | tf_op | source)
XLA Modules:
  0.0 39.3 jit_solution(1783237864529149917)
XLA Ops:
  0.0 38.3 %mlp.1 = bf16[128,4096]{1,0:T(8,128)(2,1)S(1)} custom-call(bf16[128,4096]{1,0:T(8,128)(2,1)} %x_hbm.1, bf16[4096,4096]{1,0:T(8,128)(2,1)} %wg_hbm.1, bf16[4096,4096]{1,0:T(8,128)(2,1)} %wu_hbm.1, bf16[4096,4096]{1,0:T(8,128)(2,1)} %wd_hbm.1), custom_call_target="tpu_custom_call" | custom-call | tf_op jit(solution)/shard_map/mlp/pallas_call | solution.py:303
  38.3 1.0 %copy.6 = bf16[128,4096]{1,0:T(8,128)(2,1)} copy(bf16[128,4096]{1,0:T(8,128)(2,1)S(1)} %mlp.1) | data formatting | bytes 2097152

commit v12 on v11

--- a/solution.py
+++ b/solution.py
@@ -15,33 +15,32 @@
 FH = F // 2
 KC = 512
 NK = D // KC
-XC = 256
-NR = 6
-NC = 4
+XC = 512
+NR = 3
+NC = 2
 NB = 256
 DB = 512
 TU = 128
 ND = D // DB
 NX = D // XC
-WIDTHS = (512, 512, 512, 512, 512, 512, 512, 512)
+WIDTHS = (256, 256, 512, 512, 512, 512, 512, 512, 512)
 NT = len(WIDTHS)
 OFFS = tuple(sum(WIDTHS[:j]) for j in range(NT))
 OWN_W = (512, 512, 1024, 1024, 1024)
 NS = len(OWN_W)
 OWN_O = tuple(sum(OWN_W[:j]) for j in range(NS))
-OUT_W = (1024, 1024, 1024, 512, 512)
+OUT_W = (2048, 1024, 512, 512)
 NG = len(OUT_W)
 OUT_O = tuple(sum(OUT_W[:j]) for j in range(NG))
 
 SCHEDULE = (
-    ('s',0,0), ('s',0,1), ('y',0), ('s',1,0), ('y',1), ('s',1,1), ('s',2,0), ('y',2), ('s',2,1), ('o','y0'),
-    ('y',3), ('s',3,0), ('x',0), ('s',3,1), ('y',4), ('x',1), ('o','y1'), ('y',5), ('s',4,0), ('o','x0'),
-    ('y',6), ('s',4,1), ('y',7), ('x',2), ('x',3), ('o','y2'), ('y',8), ('x',4), ('x',5), ('o','c0'), ('y',9),
-    ('o','x1'), ('o','x2'), ('o','c1'), ('t',0), ('t',1), ('s',5,0), ('s',5,1), ('e',0), ('s',6,0), ('s',6,1),
-    ('e',1), ('t',2), ('s',7,0), ('s',7,1), ('S',0), ('t',3), ('e',2), ('S',1), ('c',0), ('t',4), ('e',3),
-    ('S',2), ('c',1), ('t',5), ('e',4), ('S',3), ('c',2), ('t',6), ('e',5), ('c',3), ('t',7), ('e',6), ('c',4),
-    ('e',7), ('S',4), ('f',0), ('f',1), ('c',5), ('c',6), ('f',2), ('c',7), ('f',3), ('g',0), ('f',4), ('g',1),
-    ('f',5), ('g',2), ('f',6), ('g',3), ('f',7), ('g',4),
+    ('s',0,2), ('s',1,2), ('y',0), ('s',2,2), ('o','y0'), ('y',1), ('s',3,2), ('y',2), ('s',4,2), ('x',0),
+    ('o','y1'), ('y',3), ('o','y2'), ('x',1), ('o','x0'), ('y',4), ('o','c0'), ('x',2), ('o','x1'), ('o','c1'),
+    ('o','x2'), ('t',0), ('t',1), ('s',5,2), ('t',2), ('e',0), ('t',3), ('e',1), ('s',6,2), ('e',2), ('s',7,2),
+    ('S',0), ('e',3), ('t',4), ('S',1), ('t',5), ('c',0), ('c',1), ('e',4), ('S',2), ('c',2), ('e',5), ('t',6),
+    ('S',3), ('c',3), ('t',7), ('e',6), ('t',8), ('c',4), ('e',7), ('c',5), ('e',8), ('S',4), ('f',0), ('f',1),
+    ('f',2), ('c',6), ('c',7), ('f',3), ('f',4), ('f',5), ('g',0), ('c',8), ('f',6), ('g',1), ('f',7), ('g',2),
+    ('f',8), ('g',3),
 )
 
 
@@ -88,10 +87,10 @@
         return pltpu.make_async_remote_copy(src, dst, send, recv, device_id=peer, device_id_type=MESH)
 
     def relay_k(i, c):
-        return 2 * (i // 2) + c
+        return 2 * i + c
 
     def relay_u(i, c):
-        return 2 * relay_k(i, c) + i % 2
+        return relay_k(i, c)
 
     def y_unit(i):
         return relay_u(i, chip) if i < NR else NR + i
@@ -105,24 +104,18 @@
         return push(xo.at[u, mine], xo.at[u, mine], xx_send.at[i], xx_recv.at[i], xpeer)
 
     def d_x(m):
-        if 2 * m < NR + NC:
-            u = y_unit(2 * m)
-        else:
-            u = relay_u(2 * m - NR - NC, 1 - chip)
-        both = xo.at[pl.ds(u, 2), mine]
-        return push(both, both, dx_send.at[m], dx_recv.at[m], partner)
+        u = y_unit(m) if m < NR + NC else relay_u(m - NR - NC, 1 - chip)
+        return push(xo.at[u, mine], xo.at[u, mine], dx_send.at[m], dx_recv.at[m], partner)
 
     def on_y(i):
         y_x(i).wait_recv()
         if i < NR:
             x_x(i, chip).start()
-        if i % 2:
-            d_x(i // 2).start()
+        d_x(i).start()
 
     def on_x(i):
         x_x(i, 1 - chip).wait_recv()
-        if i % 2:
-            d_x((NR + NC + i) // 2).start()
+        d_x(NR + NC + i).start()
 
     waited = set()
 
@@ -139,7 +132,7 @@
             wd_copy(j).wait()
 
     def gate_up(xref, acc, k, lo, hi, first, h):
-        lhs = jnp.concatenate([xref[2 * k], xref[2 * k + 1]], axis=1)
+        lhs = xref[k]
         for n in range(lo, hi, NB):
             nn = pl.ds(n, NB)
             g = jnp.dot(lhs, wg[k, :, nn], preferred_element_type=F32)
@@ -169,13 +162,12 @@
     def other(slot):
         kind, r = slot[0], int(slot[1])
         if kind == "c":
-            wait_w(NR + r)
-            k = NR + r
-            ready = NR // 2 + r
+            k, ready = 2 * NR + r, NR + r
+            wait_w(k)
         else:
             wait_w(2 * r, 2 * r + 1)
-            k = relay_k(2 * r, chip if kind == "y" else 1 - chip)
-            ready = r if kind == "y" else (NR + NC) // 2 + r
+            k = relay_k(r, chip if kind == "y" else 1 - chip)
+            ready = r if kind == "y" else NR + NC + r
         d_x(ready).wait_recv()
         gate_up(xo, acc_o, k, 0, FH, slot == slots[0], h_o if slot == slots[-1] else None)
 
@@ -285,7 +277,7 @@
         y_x(i).wait_send()
     for i in range(NR):
         x_x(i, chip).wait_send()
-    for m in range(NX // 2):
+    for m in range(NX):
         d_x(m).wait_send()
     for j in range(NT):
         core_o(j).wait_send()
@@ -320,7 +312,7 @@
             pltpu.SemaphoreType.REGULAR,
             dma((2, NX)), dma((NK,)), dma((NK,)), dma((ND,)),
             dma((NR + NC,)), dma((NR + NC,)), dma((NR,)), dma((NR,)),
-            dma((NX // 2,)), dma((NX // 2,)),
+            dma((NX,)), dma((NX,)),
             dma((NT,)), dma((NT,)), dma((NT,)), dma((NT,)), dma((NS,)), dma((NS,)),
             dma((NT,)), dma((NT,)), dma((NG,)), dma((NG,)),
         ],

time: 39.4 us -> 39.4 us (level)
  no operation moved by 1% of the time
where the time goes in v12:
time: 39.4 us
  Pallas kernels  38.4 us (97%)
  local copies, waits for them, and re-layouts  0.97 us (2%)
    pallas_call x1, Pallas kernels, mlp(): pl.pallas_call(kernel, name='mlp', out_shape=pltpu.VMEM((ROWS, D), BF16),...  38.4 us
    unnamed x1, local copies, waits for them, and re-layouts  0.97 us

profile of v12, /device:TPU:0, one launch (start us, length us, event | category | flops | bytes accessed | tf_op | source)
XLA Modules:
  0.0 39.4 jit_solution(9675414398058660940)
XLA Ops:
  0.0 38.4 %mlp.1 = bf16[128,4096]{1,0:T(8,128)(2,1)S(1)} custom-call(bf16[128,4096]{1,0:T(8,128)(2,1)} %x_hbm.1, bf16[4096,4096]{1,0:T(8,128)(2,1)} %wg_hbm.1, bf16[4096,4096]{1,0:T(8,128)(2,1)} %wu_hbm.1, bf16[4096,4096]{1,0:T(8,128)(2,1)} %wd_hbm.1), custom_call_target="tpu_custom_call" | custom-call | tf_op jit(solution)/shard_map/mlp/pallas_call | solution.py:295
  38.4 1.0 %copy.6 = bf16[128,4096]{1,0:T(8,128)(2,1)} copy(bf16[128,4096]{1,0:T(8,128)(2,1)S(1)} %mlp.1) | data formatting | bytes 2097152

commit v13 on v12

--- a/solution.py
+++ b/solution.py
@@ -23,7 +23,7 @@
 TU = 128
 ND = D // DB
 NX = D // XC
-WIDTHS = (256, 256, 512, 512, 512, 512, 512, 512, 512)
+WIDTHS = (512, 512, 512, 512, 512, 512, 512, 512)
 NT = len(WIDTHS)
 OFFS = tuple(sum(WIDTHS[:j]) for j in range(NT))
 OWN_W = (512, 512, 1024, 1024, 1024)
@@ -34,13 +34,13 @@
 OUT_O = tuple(sum(OUT_W[:j]) for j in range(NG))
 
 SCHEDULE = (
-    ('s',0,2), ('s',1,2), ('y',0), ('s',2,2), ('o','y0'), ('y',1), ('s',3,2), ('y',2), ('s',4,2), ('x',0),
-    ('o','y1'), ('y',3), ('o','y2'), ('x',1), ('o','x0'), ('y',4), ('o','c0'), ('x',2), ('o','x1'), ('o','c1'),
-    ('o','x2'), ('t',0), ('t',1), ('s',5,2), ('t',2), ('e',0), ('t',3), ('e',1), ('s',6,2), ('e',2), ('s',7,2),
-    ('S',0), ('e',3), ('t',4), ('S',1), ('t',5), ('c',0), ('c',1), ('e',4), ('S',2), ('c',2), ('e',5), ('t',6),
-    ('S',3), ('c',3), ('t',7), ('e',6), ('t',8), ('c',4), ('e',7), ('c',5), ('e',8), ('S',4), ('f',0), ('f',1),
-    ('f',2), ('c',6), ('c',7), ('f',3), ('f',4), ('f',5), ('g',0), ('c',8), ('f',6), ('g',1), ('f',7), ('g',2),
-    ('f',8), ('g',3),
+    ('s',0,0), ('s',0,1), ('s',1,0), ('s',1,1), ('y',0), ('s',2,0), ('s',2,1), ('y',1), ('o','y0'), ('s',3,0),
+    ('s',3,1), ('y',2), ('s',4,0), ('x',0), ('o','y1'), ('y',3), ('o','y2'), ('x',1), ('o','x0'), ('y',4),
+    ('o','c0'), ('x',2), ('o','x1'), ('o','c1'), ('o','x2'), ('t',0), ('t',1), ('s',4,1), ('t',2), ('s',5,0),
+    ('e',0), ('s',5,1), ('s',6,0), ('e',1), ('s',6,1), ('s',7,0), ('s',7,1), ('S',0), ('e',2), ('t',3),
+    ('S',1), ('t',4), ('c',0), ('e',3), ('S',2), ('c',1), ('e',4), ('t',5), ('c',2), ('t',6), ('e',5), ('S',3),
+    ('c',3), ('t',7), ('f',0), ('e',6), ('S',4), ('c',4), ('e',7), ('c',5), ('f',1), ('c',6), ('f',2), ('f',3),
+    ('c',7), ('g',0), ('f',4), ('f',5), ('g',1), ('f',6), ('g',2), ('f',7), ('g',3),
 )
 
 

time: 39.4 us -> 38.5 us (0.977)
  Pallas kernels: 38.4 us -> 37.5 us
    pallas_call x1, Pallas kernels: 38.4 us -> 37.5 us  [mlp(): pl.pallas_call(kernel, name='mlp', out_shape=pltpu.VMEM((ROWS, D), BF16),...]
where the time goes in v13:
time: 38.5 us
  Pallas kernels  37.5 us (97%)
  local copies, waits for them, and re-layouts  0.97 us (3%)
    pallas_call x1, Pallas kernels, mlp(): pl.pallas_call(kernel, name='mlp', out_shape=pltpu.VMEM((ROWS, D), BF16),...  37.5 us
    unnamed x1, local copies, waits for them, and re-layouts  0.97 us

profile of v13, /device:TPU:0, one launch (start us, length us, event | category | flops | bytes accessed | tf_op | source)
XLA Modules:
  0.0 38.5 jit_solution(13831189525102131633)
XLA Ops:
  0.0 37.5 %mlp.1 = bf16[128,4096]{1,0:T(8,128)(2,1)S(1)} custom-call(bf16[128,4096]{1,0:T(8,128)(2,1)} %x_hbm.1, bf16[4096,4096]{1,0:T(8,128)(2,1)} %wg_hbm.1, bf16[4096,4096]{1,0:T(8,128)(2,1)} %wu_hbm.1, bf16[4096,4096]{1,0:T(8,128)(2,1)} %wd_hbm.1), custom_call_target="tpu_custom_call" | custom-call | tf_op jit(solution)/shard_map/mlp/pallas_call | solution.py:295
  37.5 1.0 %copy.6 = bf16[128,4096]{1,0:T(8,128)(2,1)} copy(bf16[128,4096]{1,0:T(8,128)(2,1)S(1)} %mlp.1) | data formatting | bytes 2097152

commit v14 on v13

--- a/solution.py
+++ b/solution.py
@@ -26,10 +26,10 @@
 WIDTHS = (512, 512, 512, 512, 512, 512, 512, 512)
 NT = len(WIDTHS)
 OFFS = tuple(sum(WIDTHS[:j]) for j in range(NT))
-OWN_W = (512, 512, 1024, 1024, 1024)
+OWN_W = (512, 512, 512, 512, 1024, 1024)
 NS = len(OWN_W)
 OWN_O = tuple(sum(OWN_W[:j]) for j in range(NS))
-OUT_W = (2048, 1024, 512, 512)
+OUT_W = (1024, 1024, 1024, 512, 512)
 NG = len(OUT_W)
 OUT_O = tuple(sum(OUT_W[:j]) for j in range(NG))
 
@@ -37,10 +37,10 @@
     ('s',0,0), ('s',0,1), ('s',1,0), ('s',1,1), ('y',0), ('s',2,0), ('s',2,1), ('y',1), ('o','y0'), ('s',3,0),
     ('s',3,1), ('y',2), ('s',4,0), ('x',0), ('o','y1'), ('y',3), ('o','y2'), ('x',1), ('o','x0'), ('y',4),
     ('o','c0'), ('x',2), ('o','x1'), ('o','c1'), ('o','x2'), ('t',0), ('t',1), ('s',4,1), ('t',2), ('s',5,0),
-    ('e',0), ('s',5,1), ('s',6,0), ('e',1), ('s',6,1), ('s',7,0), ('s',7,1), ('S',0), ('e',2), ('t',3),
-    ('S',1), ('t',4), ('c',0), ('e',3), ('S',2), ('c',1), ('e',4), ('t',5), ('c',2), ('t',6), ('e',5), ('S',3),
-    ('c',3), ('t',7), ('f',0), ('e',6), ('S',4), ('c',4), ('e',7), ('c',5), ('f',1), ('c',6), ('f',2), ('f',3),
-    ('c',7), ('g',0), ('f',4), ('f',5), ('g',1), ('f',6), ('g',2), ('f',7), ('g',3),
+    ('e',0), ('s',5,1), ('e',1), ('s',6,0), ('s',6,1), ('s',7,0), ('s',7,1), ('S',0), ('e',2), ('t',3),
+    ('S',1), ('c',0), ('t',4), ('e',3), ('S',2), ('c',1), ('t',5), ('e',4), ('t',6), ('S',3), ('c',2), ('t',7),
+    ('e',5), ('S',4), ('f',0), ('c',3), ('e',6), ('S',5), ('c',4), ('f',1), ('e',7), ('c',5), ('c',6), ('g',0),
+    ('f',2), ('c',7), ('f',3), ('f',4), ('f',5), ('g',1), ('g',2), ('f',6), ('g',3), ('f',7), ('g',4),
 )
 
 

time: 38.5 us -> 38.7 us (level)
  no operation moved by 1% of the time
where the time goes in v14:
time: 38.7 us; the launch traced here: 38.6 us
  Pallas kernels  37.6 us (97%)
  local copies, waits for them, and re-layouts  0.97 us (3%)
    pallas_call x1, Pallas kernels, mlp(): pl.pallas_call(kernel, name='mlp', out_shape=pltpu.VMEM((ROWS, D), BF16),...  37.6 us
    unnamed x1, local copies, waits for them, and re-layouts  0.97 us

profile of v14, /device:TPU:0, one launch (start us, length us, event | category | flops | bytes accessed | tf_op | source)
XLA Modules:
  0.0 38.6 jit_solution(8379538690199641726)
XLA Ops:
  0.0 37.6 %mlp.1 = bf16[128,4096]{1,0:T(8,128)(2,1)S(1)} custom-call(bf16[128,4096]{1,0:T(8,128)(2,1)} %x_hbm.1, bf16[4096,4096]{1,0:T(8,128)(2,1)} %wg_hbm.1, bf16[4096,4096]{1,0:T(8,128)(2,1)} %wu_hbm.1, bf16[4096,4096]{1,0:T(8,128)(2,1)} %wd_hbm.1), custom_call_target="tpu_custom_call" | custom-call | tf_op jit(solution)/shard_map/mlp/pallas_call | solution.py:295
  37.6 1.0 %copy.6 = bf16[128,4096]{1,0:T(8,128)(2,1)} copy(bf16[128,4096]{1,0:T(8,128)(2,1)S(1)} %mlp.1) | data formatting | bytes 2097152
